TPU v7x, 512 devices: a whole 4x8x8 slice. The times are simulated.
512 devices in a mesh: row: 32 (over z, x_lo, core), col: 16 (over y, x_hi).
Axes of the slice: x: 4 (x_hi: 2, x_lo: 2; x = x_hi * 2 + x_lo), y: 8, z: 8, core: 2. Of those that a mesh axis runs over, the one named last changes fastest.
Arguments:
- substrate: float32 [4096, 4096], P('row', 'col'), may hold values from 0.05 to 0.95
- activator: float32 [4096, 4096], P('row', 'col'), may hold values from 0 to 0.45
Outputs:
- substrate_section: float32 [4096, 4096], P('row', 'col')
- activator_section: float32 [4096, 4096], P('row', 'col')
All inputs are finite; a program needn't handle non-finite values.
Results may differ from a plain program's by a relative error of at most 0.00023.
Values sent between devices are 32-bit elements; how exact they have to be, the bound alone decides.
No kernel may reach another device: no remote copies, remote signals or barrier semaphores. Data moves between devices by JAX's collectives and lax.ppermute only.
A program may use at most 64 MiB of HBM per device.

v0:
```python
import math

import jax
import jax.numpy as jnp
from jax import lax
from jax.sharding import Mesh
from jax.sharding import PartitionSpec as P

ROW = ("row_0", "row_1", "row_2")


FEED_RATE = 0.037
KILL_RATE = 0.06
TIME_STEP = 8.0
SUBSTRATE_DIFFUSION = 4e-07
ACTIVATOR_DIFFUSION = 2e-07


def split_up(shard, dim, size):
    before, after = (shard.shape[:dim], shard.shape[dim + 1 :])
    return jnp.moveaxis(shard.reshape(*before, size, -1, *after), dim, 0)


def in_order(pieces, dim):
    pieces = jnp.moveaxis(pieces, 0, dim)
    shape = pieces.shape
    return pieces.reshape(*shape[:dim], shape[dim] * shape[dim + 1], *shape[dim + 2 :])


def moved_by_axis(pieces, axes, turns):
    shape = [lax.axis_size(a) for a in axes]
    pieces = pieces.reshape(*shape, *pieces.shape[1:])
    for k in turns:
        pieces = lax.all_to_all(pieces, axes[k], split_axis=k, concat_axis=k, tiled=True)
    return pieces.reshape(-1, *pieces.shape[len(axes) :])


def exchange_by_chip(shard, groups, turns, split_dim, concat_dim):
    size = lax.axis_size(groups[0]) * lax.axis_size(groups[1])
    pieces = split_up(shard, split_dim, size)
    return in_order(moved_by_axis(pieces, groups, turns), concat_dim)


def rotation(left_index, right_index, period, direction):
    phase_index = left_index * right_index % period
    angles = phase_index.astype(jnp.float32) * (2.0 * math.pi / period)
    return (jnp.cos(angles), direction * jnp.sin(angles))


def complex_matrix(size_count, direction):
    indices = jnp.arange(size_count, dtype=jnp.int32)
    cosine_part, sine_part = rotation(indices[:, None], indices[None, :], size_count, direction)
    return jnp.stack([jnp.stack([cosine_part, -sine_part]), jnp.stack([sine_part, cosine_part])])


def transform_last(values, direction):
    part_count, species, middle, length = values.shape
    leading = 64
    second = length // leading
    shaped = values.reshape(part_count, species, middle, leading, second)
    first_matrix = complex_matrix(leading, direction)
    first_pass = jnp.einsum(
        "pqka,qsmab->psmkb", first_matrix, shaped, precision=lax.Precision.HIGHEST
    )
    cosine_part, sine_part = rotation(
        jnp.arange(leading, dtype=jnp.int32)[:, None],
        jnp.arange(second, dtype=jnp.int32)[None, :],
        length,
        direction,
    )
    turned = jnp.stack(
        [
            first_pass[0] * cosine_part - first_pass[1] * sine_part,
            first_pass[0] * sine_part + first_pass[1] * cosine_part,
        ]
    )
    second_matrix = complex_matrix(second, direction)
    second_pass = jnp.einsum(
        "pqkb,qsmjb->psmkj", second_matrix, turned, precision=lax.Precision.HIGHEST
    )
    return second_pass.reshape(part_count, species, middle, length)


def signed_squares(wave_index, total):
    signed = jnp.where(2 * wave_index < total, wave_index, wave_index - total).astype(jnp.float32)
    angular = 2.0 * math.pi * signed
    return angular * angular


def section_factors(row_wave, col_wave, total_rows, total_cols):
    wave_number = signed_squares(row_wave, total_rows) + signed_squares(col_wave, total_cols)
    normalize = 1.0 / (total_rows * total_cols)
    growths = []
    forcings = []
    for diffusion, decay_rate in (
        (SUBSTRATE_DIFFUSION, FEED_RATE),
        (ACTIVATOR_DIFFUSION, FEED_RATE + KILL_RATE),
    ):
        linear = -diffusion * wave_number - decay_rate
        exponent = linear * (0.5 * TIME_STEP)
        growths.append(jnp.exp(exponent) * normalize)
        forcings.append(jnp.expm1(exponent) / linear * normalize)
    return (jnp.stack(growths), jnp.stack(forcings))


def advance(spectra, growth, forcing):
    real_part = spectra[0]
    imag_part = spectra[1]
    return jnp.stack(
        [growth * real_part + forcing * imag_part, growth * imag_part - forcing * real_part]
    )


def col_forward(values):
    return lax.all_to_all(values, "col", split_axis=2, concat_axis=3, tiled=True)


def col_backward(values):
    return lax.all_to_all(values, "col", split_axis=3, concat_axis=2, tiled=True)


def row_forward(values):
    return lax.all_to_all(values, ROW, split_axis=2, concat_axis=3, tiled=True)


def row_backward(values):
    return exchange_by_chip(values, (("row_0", "row_1"), "row_2"), (1, 0), 3, 2)


def on_device(substrate, activator):
    row_count, col_count = substrate.shape
    total_rows = row_count * lax.axis_size(ROW)
    total_cols = col_count * lax.axis_size("col")
    row_index = lax.axis_index(ROW)
    col_index = lax.axis_index("col")
    reaction = substrate * activator * activator
    fields = jnp.stack(
        [jnp.stack([substrate, activator]), jnp.stack([FEED_RATE - reaction, reaction])]
    )
    spectra = transform_last(col_forward(fields), -1)
    spectra = row_forward(col_forward(jnp.swapaxes(spectra, 2, 3)))
    spectra = transform_last(spectra, -1)
    local_cols = col_count // lax.axis_size(ROW)
    col_wave = (
        col_count * col_index
        + local_cols * row_index
        + jnp.arange(local_cols, dtype=jnp.int32)[:, None]
    )
    row_wave = jnp.arange(total_rows, dtype=jnp.int32)[None, :]
    growth, forcing = section_factors(row_wave, col_wave, total_rows, total_cols)
    spectra = transform_last(advance(spectra, growth, forcing), 1)
    spectra = col_backward(row_backward(spectra))
    spectra = jnp.swapaxes(spectra, 2, 3)
    spectra = transform_last(spectra, 1)
    fields = lax.all_to_all(spectra[:1], "col", split_axis=3, concat_axis=2, tiled=True)
    return (fields[0, 0], fields[0, 1])


def solution(mesh):
    split = Mesh(
        mesh.devices.reshape(8, 2, 2, mesh.shape["col"]), ("row_0", "row_1", "row_2", "col")
    )
    placed = (P(ROW, "col"), P(ROW, "col"))
    return jax.shard_map(
        on_device,
        mesh=split,
        in_specs=placed,
        out_specs=(P(ROW, "col"), P(ROW, "col")),
        check_vma=False,
    )
```

profile of v0, /device:TPU:1, one launch (start us, length us, event | category | flops | bytes accessed | tf_op | source)
XLA Modules:
  0.0 238.1 jit_solution(18441862085176898476)
XLA Ops:
  5.4 10.2 %all-to-all-start = ((f32[2,2,128,256]{3,1,0,2:T(2,128)}), f32[2,2,128,256]{3,1,0,2:T(2,128)S(1)}, u32[]{:S(2)}, u32[]{:S(2)}) async-start(f32[2,2,128,256]{3,1,0,2:T(2,128)} %pad_maximum_fusion.1), calls=%async_computation | async-start | bytes 1048576 | tf_op jit(solution)/shard_map/all_to_all | solution.py:115
  16.2 16.6 %all-to-all-done = f32[2,2,128,256]{3,1,0,2:T(2,128)S(1)} async-done(((f32[2,2,128,256]{3,1,0,2:T(2,128)}), f32[2,2,128,256]{3,1,0,2:T(2,128)S(1)}, u32[]{:S(2)}, u32[]{:S(2)}) %all-to-all-start) | async-done | bytes 524320 | tf_op jit(solution)/shard_map/all_to_all | solution.py:115
  35.3 1.8 convolution_bitcast_fusion.6
  37.8 8.2 %copy.66 = f32[2,2,4096,8]{3,1,0,2:T(2,128)} copy(f32[2,2,4096,8]{2,3,1,0:T(8,128)S(1)} %bitcast.164) | data formatting | bytes 1048576 | tf_op jit(solution)/shard_map/transpose | solution.py:141
  46.0 14.9 %reshape.444 = f32[16,1,8192]{2,1,0:T(1,128)S(1)} reshape(f32[4096,2,2,8]{3,2,1,0:T(2,128)} %bitcast.160) | data formatting | bytes 1048576
  61.0 21.9 %all_to_all.94 = f32[16,1,8192]{2,1,0:T(1,128)S(1)} all-to-all(f32[16,1,8192]{2,1,0:T(1,128)S(1)} %reshape.444), channel_id=1, replica_groups=mesh['row_0'=8,'row_1'=2,'row_2'=2,'col'=16] {'col'}, dimensions={0} | all-to-all | bytes 1048576 | tf_op jit(solution)/shard_map/all_to_all | solution.py:115
  83.3 1.9 reduce
  85.2 14.7 %reshape.445 = f32[4096,2,2,8]{3,2,1,0:T(2,128)} reshape(f32[16,8192]{1,0:T(8,128)S(1)} %reduce) | data formatting | bytes 1048576
  100.0 9.5 %copy.67 = f32[2,2,4096,8]{2,3,1,0:T(8,128)S(1)} copy(f32[2,2,4096,8]{3,1,0,2:T(2,128)} %bitcast.161) | data formatting | bytes 1048576 | tf_op jit(solution)/shard_map/all_to_all | solution.py:115
  110.5 13.2 %all-to-all-start.2 = ((f32[2,2,256,128]{3,1,0,2:T(2,128)}), f32[2,2,256,128]{3,1,0,2:T(2,128)S(1)}, u32[]{:S(2)}, u32[]{:S(2)}) async-start(f32[2,2,256,128]{3,1,0,2:T(2,128)} %copy.68), calls=%async_computation.2 | async-start | bytes 1048576 | tf_op jit(solution)/shard_map/all_to_all | solution.py:123
  124.3 16.0 %all-to-all-done.2 = f32[2,2,256,128]{3,1,0,2:T(2,128)S(1)} async-done(((f32[2,2,256,128]{3,1,0,2:T(2,128)}), f32[2,2,256,128]{3,1,0,2:T(2,128)S(1)}, u32[]{:S(2)}, u32[]{:S(2)}) %all-to-all-start.2) | async-done | bytes 524320 | tf_op jit(solution)/shard_map/all_to_all | solution.py:123
  140.6 1.8 convolution_bitcast_fusion.5
  142.6 1.8 convolution_bitcast_fusion.4
  145.9 1.8 convolution_bitcast_fusion.2
  148.3 5.1 %all_to_all.95 = f32[16,2,2,2,8,128]{5,0,4,3,2,1:T(8,128)S(1)} all-to-all(f32[16,2,2,2,8,128]{5,0,4,3,2,1:T(8,128)S(1)} %copy.75), channel_id=1, replica_groups=mesh['row_0'=8,'row_1'=2,'row_2'=2,'col'=16] {'row_2'}, dimensions={1} | all-to-all | bytes 1048576 | tf_op jit(solution)/shard_map/all_to_all | solution.py:34
  153.9 18.7 %all_to_all.96 = f32[16,2,2,2,8,128]{5,1,4,3,2,0:T(2,128)S(1)} all-to-all(f32[16,2,2,2,8,128]{5,1,4,3,2,0:T(2,128)S(1)} %copy.76), channel_id=1, replica_groups=mesh['row_0'=8,'row_1'=2,'row_2'=2,'col'=16] {'row_0','row_1'}, dimensions={0} | all-to-all | bytes 1048576 | tf_op jit(solution)/shard_map/all_to_all | solution.py:34
  172.9 17.8 %all_to_all.97 = f32[2,2,256,128]{2,1,0,3:T(2,128)S(1)} all-to-all(f32[2,2,256,128]{2,1,0,3:T(2,128)S(1)} %copy.78), channel_id=1, replica_groups=mesh['row_0'=8,'row_1'=2,'row_2'=2,'col'=16] {'col'}, dimensions={3} | all-to-all | bytes 1048576 | tf_op jit(solution)/shard_map/all_to_all | solution.py:119
  191.2 1.8 convolution_bitcast_fusion.1
  193.2 1.8 convolution_bitcast_fusion
  195.1 4.8 %copy.117 = f32[1,2,8,64,64]{2,1,4,3,0:T(2,128)} copy(f32[1,2,8,64,64]{3,4,0,2,1:T(8,128)S(1)} %slice.76) | data formatting | bytes 524288 | tf_op jit(solution)/shard_map/slice | solution.py:155
  199.9 8.3 %reshape.446 = f32[16,1,4096]{2,1,0:T(1,128)S(1)} reshape(f32[4096,1,2,8]{3,2,1,0:T(2,128)} %bitcast.162) | data formatting | bytes 524288
  208.2 15.2 %all_to_all.98 = f32[16,1,4096]{2,1,0:T(1,128)S(1)} all-to-all(f32[16,1,4096]{2,1,0:T(1,128)S(1)} %reshape.446), channel_id=1, replica_groups=mesh['row_0'=8,'row_1'=2,'row_2'=2,'col'=16] {'col'}, dimensions={0} | all-to-all | bytes 524288 | tf_op jit(solution)/shard_map/all_to_all | solution.py:155
  224.6 7.7 %reshape.447 = f32[4096,1,2,8]{3,2,1,0:T(2,128)} reshape(f32[16,4096]{1,0:T(8,128)S(1)} %reduce.1) | data formatting | bytes 524288
  232.3 5.1 %copy.84 = f32[1,2,16,8,256]{4,3,2,1,0:T(8,128)S(1)} copy(f32[1,2,16,8,256]{3,1,4,2,0:T(2,128)} %bitcast.163) | data formatting | bytes 524288 | tf_op jit(solution)/shard_map/all_to_all | solution.py:155
  (43 shorter events, 16.4 us)
Async XLA Ops:
  5.4 27.4 %all-to-all-start = ((f32[2,2,128,256]{3,1,0,2:T(2,128)}), f32[2,2,128,256]{3,1,0,2:T(2,128)S(1)}, u32[]{:S(2)}, u32[]{:S(2)}) async-start(f32[2,2,128,256]{3,1,0,2:T(2,128)} %pad_maximum_fusion.1), calls=%async_computation | async-start | bytes 1048576 | tf_op jit(solution)/shard_map/all_to_all | solution.py:115
  110.5 29.8 %all-to-all-start.2 = ((f32[2,2,256,128]{3,1,0,2:T(2,128)}), f32[2,2,256,128]{3,1,0,2:T(2,128)S(1)}, u32[]{:S(2)}, u32[]{:S(2)}) async-start(f32[2,2,256,128]{3,1,0,2:T(2,128)} %copy.68), calls=%async_computation.2 | async-start | bytes 1048576 | tf_op jit(solution)/shard_map/all_to_all | solution.py:123
where the time goes:
time: 241 us; the launch traced here: 238 us
  local copies, waits for them, and re-layouts  81 us (34%)
  blocking collectives  78.7 us (33%)
  waiting for transfers between devices  32.6 us (14%)
  starting transfers between devices  23.4 us (10%)
  matrix products  13.7 us (6%)
  other arithmetic  7.65 us (3%)
    unnamed x4, local copies, waits for them, and re-layouts  45.6 us
    all_to_all x2, blocking collectives, moved_by_axis(): lax.all_to_all(pieces, axes[k], split_axis=k, concat_axis=k, tiled=True)  23.8 us
    all_to_all x1, blocking collectives, col_forward(): lax.all_to_all(values, 'col', split_axis=2, concat_axis=3, tiled=True)  21.9 us
    all_to_all x1, blocking collectives, col_backward(): lax.all_to_all(values, 'col', split_axis=3, concat_axis=2, tiled=True)  17.8 us
    all_to_all x1, waiting for transfers between devices, col_forward(): lax.all_to_all(values, 'col', split_axis=2, concat_axis=3, tiled=True)  16.6 us
    all_to_all x1, waiting for transfers between devices, row_forward(): return lax.all_to_all(values, ROW, split_axis=2, concat_axis=3, tiled=True)  16 us
    all_to_all x1, blocking collectives, on_device(): lax.all_to_all(spectra[:1], 'col', split_axis=3, concat_axis=2, tiled=True)  15.2 us
    all_to_all x1, starting transfers between devices, row_forward(): return lax.all_to_all(values, ROW, split_axis=2, concat_axis=3, tiled=True)  13.2 us
  transfers between devices with their start and end apart: 2, of which 2 were waited for; matrix products, arithmetic and copies ran while one was open for 0% of the time, Pallas kernels for 0%

commit v1 on v0

v1 whole, which is shorter than its diff:
```python
import math

import jax
import jax.numpy as jnp
import numpy as np
from jax import lax
from jax.experimental import pallas as pl
from jax.experimental.pallas import tpu as pltpu
from jax.sharding import Mesh
from jax.sharding import PartitionSpec as P

ROW = ("row_0", "row_1", "row_2")
ALL = ("row_0", "row_1", "row_2", "col")

FEED_RATE = 0.037
KILL_RATE = 0.06
TIME_STEP = 8.0
SUBSTRATE_DIFFUSION = 4e-07
ACTIVATOR_DIFFUSION = 2e-07

N = 4096
R = 32
C = 16
I = 8
M = 256
D = R * C
LANES = 128


def add(a, b):
    return b if a is None else a if b is None else a + b


def sub(a, b):
    return (None if b is None else -b) if a is None else a if b is None else a - b


def scale(a, c):
    if a is None or c == 0.0:
        return None
    return a if c == 1.0 else -a if c == -1.0 else a * c


def turn(z, k, n, sign):
    c, s = unit(k, n, sign)
    return sub(scale(z[0], c), scale(z[1], s)), add(scale(z[0], s), scale(z[1], c))


def unit(k, n, sign):
    quarter, rest = divmod(4 * (k % n), n)
    if rest == 0:
        c, s = ((1.0, 0.0), (0.0, 1.0), (-1.0, 0.0), (0.0, -1.0))[quarter]
    else:
        c, s = math.cos(2 * math.pi * k / n), math.sin(2 * math.pi * k / n)
    return c, sign * s


def dft(values, sign):
    n = len(values)
    if n == 1:
        return values
    even, odd = dft(values[0::2], sign), dft(values[1::2], sign)
    odd = [turn(z, k, n, sign) for k, z in enumerate(odd)]
    pairs = list(zip(even, odd))
    return [(add(e[0], o[0]), add(e[1], o[1])) for e, o in pairs] + [
        (sub(e[0], o[0]), sub(e[1], o[1])) for e, o in pairs
    ]


def real_dft(values):
    n = len(values)
    if n == 2:
        return [(add(*values), None), (sub(*values), None)]
    even, odd = real_dft(values[0::2]), real_dft(values[1::2])
    odd = [turn(z, k, n, -1) for k, z in enumerate(odd)]
    low = [(add(e[0], o[0]), add(e[1], o[1])) for e, o in zip(even, odd)]
    high = [(sub(e[0], o[0]), sub(o[1], e[1])) for e, o in zip(even, odd)]
    return low + high[: n // 4][::-1]


def dot(a, b, dims=((1,), (0,))):
    return lax.dot_general(
        a, b, (dims, ((), ())), precision=lax.Precision.HIGHEST, preferred_element_type=jnp.float32
    )


def lane_of(shape):
    return lax.broadcasted_iota(jnp.int32, shape, len(shape) - 1)


def y_forward(fields, cos_y, sin_y, matrix, out, turned):
    for f in range(3):
        lines = []
        for c in range(C):
            if f < 2:
                lines.append(fields[c, f * I : (f + 1) * I, :])
            else:
                a = fields[c, I:, :]
                lines.append(fields[c, :I, :] * a * a)
        half = real_dft(lines)
        for k in range(C):
            re, im = half[k] if k <= C // 2 else half[C - k]
            if im is not None and k > C // 2:
                im = -im
            if k:
                c, s = cos_y[k : k + 1, :], sin_y[k : k + 1, :]
                if im is None:
                    re, im = re * c, -re * s
                else:
                    re, im = re * c + im * s, im * c - re * s
            else:
                im = jnp.zeros_like(re)
            row = k * 32 + f * I
            turned[row : row + I, :M] = re
            turned[row : row + I, M:] = im
    for k in range(C):
        row = k * 32 + 3 * I
        turned[row : row + I, :] = jnp.zeros((I, 2 * M), jnp.float32)
    lane = lane_of((R, LANES))
    for t in range(4):
        half = dot(matrix[...], turned[t * LANES : (t + 1) * LANES, :], ((1,), (1,)))
        for part in range(2):
            blocks = [half[part * 128 + 32 * s : part * 128 + 32 * (s + 1), :] for s in range(4)]
            if t == 0 and part == 1:
                first = (lax.broadcasted_iota(jnp.int32, (R, LANES), 0) == 0) & (lane < 32)
                blocks[0] = jnp.where(first, half[256:257, :], blocks[0])
            for j in range(4):
                piece = None
                for s in range(4):
                    moved = blocks[s] if s == j else pltpu.roll(blocks[s], 32 * (s - j) % LANES, 1)
                    piece = moved if piece is None else jnp.where(lane >= 32 * s, moved, piece)
                out[pl.ds((4 * t + j) * 2 + part, R, stride=2 * C), :] = piece


def x_section(first, lines, cos_c, sin_c, cos_i, sin_i, forward, backward, growth, forcing, out, a_re, a_im, wide):
    for h in range(2):
        values = [
            (
                lines[pl.ds(32 * r + 16 * h, 8, stride=2), :],
                lines[pl.ds(32 * r + 16 * h + 1, 8, stride=2), :],
            )
            for r in range(R)
        ]
        for k, (re, im) in enumerate(dft(values, -1)):
            a_re[k * C + 8 * h : k * C + 8 * h + 8, :] = re
            a_im[k * C + 8 * h : k * C + 8 * h + 8, :] = im
    for h in range(4):
        values = []
        for c in range(C):
            rows = slice(c * R + 8 * h, c * R + 8 * h + 8)
            re, im = a_re[pl.ds(8 * h * C + c, 8, stride=C), :], a_im[pl.ds(8 * h * C + c, 8, stride=C), :]
            u, v = cos_c[rows, :], sin_c[rows, :]
            values.append((re * u + im * v, im * u - re * v))
        for k, (re, im) in enumerate(dft(values, -1)):
            rows = slice(k * R + 8 * h, k * R + 8 * h + 8)
            u, v = cos_i[rows, :], sin_i[rows, :]
            wide[rows, :LANES] = re * u + im * v
            wide[rows, LANES:] = im * u - re * v
    spectra = dot(wide[...], forward[...])
    g, f = growth[...], forcing[...]
    wide[:, :LANES] = g * spectra[:, :LANES] + f * spectra[:, 2 * LANES : 3 * LANES]
    wide[:, LANES:] = g * spectra[:, LANES : 2 * LANES] + f * spectra[:, 3 * LANES :]
    wide[...] = dot(wide[...], backward[...])
    for h in range(4):
        values = []
        for k in range(C):
            rows = slice(k * R + 8 * h, k * R + 8 * h + 8)
            re, im = wide[rows, :LANES], wide[rows, LANES:]
            u, v = cos_i[rows, :], sin_i[rows, :]
            values.append((re * u - im * v, im * u + re * v))
        for c, (re, im) in enumerate(dft(values, 1)):
            rows = slice(c * R + 8 * h, c * R + 8 * h + 8)
            u, v = cos_c[rows, :], sin_c[rows, :]
            a_re[pl.ds(8 * h * C + c, 8, stride=C), :] = re * u - im * v
            a_im[pl.ds(8 * h * C + c, 8, stride=C), :] = im * u + re * v
    lane = lane_of((8, LANES))
    packed = (lane < 80) & (first[0] == 1)
    for h in range(2):
        values = [
            (a_re[k * C + 8 * h : k * C + 8 * h + 8, :], a_im[k * C + 8 * h : k * C + 8 * h + 8, :])
            for k in range(R)
        ]
        for r, (re, im) in enumerate(dft(values, 1)):
            im = jnp.where(packed, im, pltpu.roll(im, 64, 1))
            out[r * C + 8 * h : r * C + 8 * h + 8, :] = jnp.where(lane < 64, re, im)


def y_backward(pieces, constant, cos_y, sin_y, matrix, out, spectrum, turned):
    lane = lane_of((R, LANES))
    for t in range(2):
        sources = [pieces[pl.ds(8 * t + j, R, stride=C), :] for j in range(8)]
        for b in range(8):
            block = None
            for j in range(8):
                moved = sources[j] if j == b else pltpu.roll(sources[j], 16 * (j - b) % LANES, 1)
                block = moved if block is None else jnp.where(lane >= 16 * j, moved, block)
            spectrum[b * R : (b + 1) * R, t * LANES : (t + 1) * LANES] = block
    flipped = spectrum[...].T
    turned[...] = dot(flipped, matrix[...])
    parity = 1.0 - 2.0 * (lane_of((16, M)) % 2).astype(jnp.float32)
    values = []
    for k in range(C):
        re, im = turned[16 * k : 16 * (k + 1), :M], turned[16 * k : 16 * (k + 1), M:]
        if k == 0:
            re, im = re - flipped[:16, 0:1] + flipped[:16, 128:129] * parity, None
        else:
            u, v = cos_y[k : k + 1, :], sin_y[k : k + 1, :]
            re, im = re * u - im * v, im * u + re * v
        values.append((re, im))
    substrate_row = lax.broadcasted_iota(jnp.int32, (16, M), 0) < I
    shift = jnp.where(substrate_row, constant[0], 0.0)
    for c, (re, _) in enumerate(dft(values, 1)):
        out[c] = re + shift


def tables():
    f32 = np.float32
    angle = 2 * np.pi / N * (np.arange(C)[:, None] * np.arange(M)[None, :])
    cos_y, sin_y = np.cos(angle), np.sin(angle)
    turn_m = 2 * np.pi / M * (np.arange(128)[:, None] * np.arange(M)[None, :] % M)
    c, s = np.cos(turn_m), np.sin(turn_m)
    last = np.zeros((8, 2 * M))
    last[0, :M] = 1 - 2 * (np.arange(M) % 2)
    y_matrix = np.concatenate([np.block([[c, s], [-s, c]]), last])
    y_inverse = 2 * np.block([[c, s], [-s, c]])
    k_r = np.tile(np.arange(R), C)
    outer = np.repeat(np.arange(C), R)
    ones = np.ones((1, LANES))
    angle = 2 * np.pi / D * (outer * k_r % D)[:, None] * ones
    cos_c, sin_c = np.cos(angle), np.sin(angle)
    angle = 2 * np.pi / N * ((k_r + R * outer)[:, None] * (np.arange(LANES) % I)[None, :] % N)
    cos_i, sin_i = np.cos(angle), np.sin(angle)
    angle = 2 * np.pi / I * (np.arange(I)[:, None] * np.arange(I)[None, :] % I)
    c, s = np.cos(angle), np.sin(angle)
    forward = np.zeros((2, LANES, 2, 2, LANES))
    backward = np.zeros((2, LANES, 2, LANES))
    for slot in range(5):
        for field in range(2):
            here = slice(16 * slot + I * field, 16 * slot + I * field + I)
            backward[0, here, 0, here], backward[1, here, 0, here] = c, -s
            backward[0, here, 1, here], backward[1, here, 1, here] = s, c
            for kind, taken in enumerate((field, 2)):
                start = 32 * (slot % 4) + I * taken
                there = slice(start, start + I)
                forward[0, there, kind, 0, here], forward[1, there, kind, 0, here] = c, s
                forward[0, there, kind, 1, here], forward[1, there, kind, 1, here] = -s, c
    forward = forward.reshape(2 * LANES, 4 * LANES)
    backward = backward.reshape(2 * LANES, 2 * LANES)
    both = (cos_y, sin_y, y_matrix, y_inverse, cos_c, sin_c, cos_i, sin_i, forward, backward)
    return [a.astype(f32) for a in both]


def signed_squares(wave_index):
    signed = jnp.where(2 * wave_index < N, wave_index, wave_index - N).astype(jnp.float32)
    angular = 2.0 * math.pi * signed
    return angular * angular


def factors(row_index, col_index):
    row = lax.broadcasted_iota(jnp.int32, (D, LANES), 0)
    lane = lane_of((D, LANES))
    p = row % R + R * (row // R) + D * (lane % I)
    slot = lane // 16
    q = jnp.where(slot == 4, N // 2, col_index + C * (R * (slot % 4) + row_index))
    wave_number = signed_squares(p) + signed_squares(q)
    substrate = lane // I % 2 == 0
    diffusion = jnp.where(substrate, SUBSTRATE_DIFFUSION, ACTIVATOR_DIFFUSION)
    decay = jnp.where(substrate, FEED_RATE, FEED_RATE + KILL_RATE)
    linear = -diffusion * wave_number - decay
    exponent = linear * (0.5 * TIME_STEP)
    normalize = 1.0 / (N * N)
    growth = jnp.exp(exponent) * normalize
    forcing = jnp.expm1(exponent) / linear * jnp.where(substrate, -normalize, normalize)
    return growth, forcing


def call(body, out_shape, scratch, *operands, scalars=0):
    spaces = [pl.BlockSpec(memory_space=pltpu.SMEM if k < scalars else pltpu.VMEM) for k in range(len(operands))]
    return pl.pallas_call(
        body,
        out_shape=jax.ShapeDtypeStruct(out_shape, jnp.float32),
        in_specs=spaces,
        out_specs=pl.BlockSpec(memory_space=pltpu.VMEM),
        scratch_shapes=[pltpu.VMEM(shape, jnp.float32) for shape in scratch],
        compiler_params=pltpu.CompilerParams(vmem_limit_bytes=48 * 1024 * 1024),
    )(*operands)


def y_backward_body(constant, pieces, *rest):
    return y_backward(pieces, constant, *rest)


def on_device(substrate, activator):
    cos_y, sin_y, y_matrix, y_inverse, cos_c, sin_c, cos_i, sin_i, forward, backward = tables()
    row_index = lax.axis_index(ROW)
    col_index = lax.axis_index("col")
    growth, forcing = factors(row_index, col_index)
    first = ((row_index == 0) & (col_index == 0)).astype(jnp.int32).reshape(1)
    rate = jnp.full((1,), -FEED_RATE, jnp.float32)
    constant = jnp.expm1(rate * (0.5 * TIME_STEP)) / rate * FEED_RATE

    fields = jnp.concatenate([substrate.reshape(C, I, M), activator.reshape(C, I, M)], axis=1)
    fields = lax.all_to_all(fields, "col", 0, 0, tiled=True)
    pieces = call(y_forward, (2 * D, LANES), [(512, 2 * M)], fields, cos_y, sin_y, y_matrix)
    lines = lax.all_to_all(pieces.reshape(D, 2, LANES), ALL, 0, 0, tiled=True).reshape(2 * D, LANES)
    pieces = call(
        x_section,
        (D, LANES),
        [(D, LANES), (D, LANES), (D, 2 * LANES)],
        first,
        lines,
        cos_c,
        sin_c,
        cos_i,
        sin_i,
        forward,
        backward,
        growth,
        forcing,
        scalars=1,
    )
    pieces = lax.all_to_all(pieces.reshape(D, 1, LANES), ALL, 0, 0, tiled=True).reshape(D, LANES)
    fields = call(
        y_backward_body, (C, 2 * I, M), [(M, M), (M, 2 * M)], constant, pieces, cos_y, sin_y, y_inverse, scalars=1
    )
    fields = lax.all_to_all(fields, "col", 0, 0, tiled=True)
    return (fields[:, :I].reshape(C * I, M), fields[:, I:].reshape(C * I, M))


def solution(mesh):
    split = Mesh(
        mesh.devices.reshape(8, 2, 2, mesh.shape["col"]), ("row_0", "row_1", "row_2", "col")
    )
    placed = (P(ROW, "col"), P(ROW, "col"))
    return jax.shard_map(on_device, mesh=split, in_specs=placed, out_specs=placed, check_vma=False)
```

time: 241 us -> 113 us (0.47)
  local copies, waits for them, and re-layouts: 81 us -> 0.77 us
  blocking collectives: 78.7 us -> 40.9 us
  matrix products: 13.7 us -> 0 us
  Pallas kernels: 0 us -> 7.53 us
  other arithmetic: 7.65 us -> 2.29 us
  starting transfers between devices: 23.4 us -> 26.4 us
    unnamed x4 -> x20, local copies, waits for them, and re-layouts: 45.6 us -> 0.05 us
    all_to_all x5 -> x2, blocking collectives: 78.7 us -> 40.9 us  [the longest x1 26 us: on_device(): lax.all_to_all(pieces.reshape(D, 1, LANES), ALL, 0, 0, tiled=True)]
    all_to_all x10 -> x0, local copies, waits for them, and re-layouts: 17.1 us -> none  [the longest x4 11.3 us: col_forward(): lax.all_to_all(values, 'col', split_axis=2, concat_axis=3, tiled=True)]
    dot_general x8 -> x0, matrix products: 13.7 us -> none  [the longest x4 7.28 us: transform_last(): jnp.einsum('pqkb,qsmjb->psmkj', second_matrix, turned, precision=lax.Prec...]
    transpose x3 -> x0, local copies, waits for them, and re-layouts: 8.84 us -> none  [the longest x1 8.18 us: on_device(): spectra = row_forward(col_forward(jnp.swapaxes(spectra, 2, 3)))]
    pallas_call x0 -> x3, Pallas kernels: none -> 7.53 us  [call(): pl.pallas_call(body, out_shape=jax.ShapeDtypeStruct(out_shape, jnp.float3...]
    slice x2 -> x0, local copies, waits for them, and re-layouts: 4.8 us -> none  [on_device(): spectra[:1]]
    all_to_all x2 -> x0, other arithmetic: 3.15 us -> none  [the longest x1 1.89 us: col_forward(): lax.all_to_all(values, 'col', split_axis=2, concat_axis=3, tiled=True)]
where the time goes in v1:
time: 113 us
  blocking collectives  40.9 us (36%)
  waiting for transfers between devices  33.8 us (30%)
  starting transfers between devices  26.4 us (23%)
  Pallas kernels  7.53 us (7%)
  other arithmetic  2.29 us (2%)
    all_to_all x1, blocking collectives, on_device(): lax.all_to_all(pieces.reshape(D, 1, LANES), ALL, 0, 0, tiled=True)  26 us
    all_to_all x1, waiting for transfers between devices, on_device(): lax.all_to_all(pieces.reshape(D, 2, LANES), ALL, 0, 0, tiled=True)  21.8 us
    all_to_all x1, starting transfers between devices, on_device(): lax.all_to_all(pieces.reshape(D, 2, LANES), ALL, 0, 0, tiled=True)  16 us
    all_to_all x1, blocking collectives, on_device(): fields = lax.all_to_all(fields, 'col', 0, 0, tiled=True)  14.9 us
    all_to_all x1, waiting for transfers between devices, on_device(): fields = lax.all_to_all(fields, 'col', 0, 0, tiled=True)  12 us
    all_to_all x1, starting transfers between devices, on_device(): fields = lax.all_to_all(fields, 'col', 0, 0, tiled=True)  10.3 us
    pallas_call x3, Pallas kernels, call(): pl.pallas_call(body, out_shape=jax.ShapeDtypeStruct(out_shape, jnp.float3...  7.53 us
  transfers between devices with their start and end apart: 2, of which 2 were waited for; matrix products, arithmetic and copies ran while one was open for 0% of the time, Pallas kernels for 0%

profile of v1, /device:TPU:1, one launch (start us, length us, event | category | flops | bytes accessed | tf_op | source)
XLA Modules:
  0.0 112.5 jit_solution(9328765994164685987)
XLA Ops:
  0.6 0.0 copy-start
  0.6 1.7 %pad_maximum_fusion = f32[16,16,256]{2,1,0:T(8,128)} fusion(f32[16,8,256]{2,1,0:T(8,128)} %bitcast.16, f32[16,8,256]{2,1,0:T(8,128)} %bitcast.17), kind=kLoop, calls=%fused_computation.30 | loop fusion | flops 65536 | bytes 524288 | tf_op jit(solution)/shard_map/concatenate | solution.py:302
  2.4 10.3 %all-to-all-start = ((f32[16,16,256]{2,1,0:T(8,128)}), f32[16,16,256]{2,1,0:T(8,128)S(1)}, u32[]{:S(2)}, u32[]{:S(2)}) async-start(f32[16,16,256]{2,1,0:T(8,128)} %pad_maximum_fusion), calls=%async_computation | async-start | bytes 524288 | tf_op jit(solution)/shard_map/all_to_all | solution.py:303
  12.7 0.0 copy-start.8
  12.8 12.0 %all-to-all-done.fields = f32[16,16,256]{2,1,0:T(8,128)S(1)} async-done(((f32[16,16,256]{2,1,0:T(8,128)}), f32[16,16,256]{2,1,0:T(8,128)S(1)}, u32[]{:S(2)}, u32[]{:S(2)}) %all-to-all-start) | async-done | bytes 262176 | tf_op jit(solution)/shard_map/all_to_all | solution.py:303
  24.8 0.0 copy-done
  24.8 0.0 copy-done.9
  24.8 0.0 copy-done.8
  24.8 0.0 copy-start.7
  24.8 3.2 %shard_map.131 = f32[1024,128]{1,0:T(8,128)} custom-call(f32[16,16,256]{2,1,0:T(8,128)S(1)} %all-to-all-done.fields, f32[16,256]{1,0:T(8,128)S(1)} %copy-done.9, f32[16,256]{1,0:T(8,128)S(1)} %copy-done.8, f32[264,512]{1,0:T(8,128)S(1)} %copy-done), custom_call_target="tpu_custom_call" | custom-call | tf_op jit(solution)/shard_map/pallas_call | solution.py:279
  28.0 16.0 %all-to-all-start.1 = ((f32[512,2,128]{2,1,0:T(2,128)}), f32[512,2,128]{2,1,0:T(2,128)S(1)}, u32[]{:S(2)}, u32[]{:S(2)}) async-start(f32[512,2,128]{2,1,0:T(2,128)} %bitcast.3), calls=%async_computation.1 | async-start | bytes 1048576 | tf_op jit(solution)/shard_map/all_to_all | solution.py:305
  44.0 0.0 copy-start.2
  44.2 0.5 select_multiply_fusion
  44.7 21.8 %all-to-all-done.1 = f32[512,2,128]{2,1,0:T(2,128)S(1)} async-done(((f32[512,2,128]{2,1,0:T(2,128)}), f32[512,2,128]{2,1,0:T(2,128)S(1)}, u32[]{:S(2)}, u32[]{:S(2)}) %all-to-all-start.1) | async-done | bytes 524320 | tf_op jit(solution)/shard_map/all_to_all | solution.py:305
  66.5 0.0 copy-done.7
  66.5 0.0 copy-done.5
  66.5 0.0 copy-done.6
  66.5 0.0 copy-done.2
  66.5 3.2 %shard_map.132 = f32[512,128]{1,0:T(8,128)S(1)} custom-call(s32[1]{0:T(128)} %bitcast.first, f32[1024,128]{1,0:T(8,128)S(1)} %bitcast.13, f32[512,128]{1,0:T(8,128)S(1)} %copy-done.7, f32[512,128]{1,0:T(8,128)S(1)} %copy-done.6, f32[512,128]{1,0:T(8,128)S(1)} %copy-done.5, f32[512,128]{1,0:T(8,128)S(1)} %copy-done.4, f32[256,512]{1,0:T(8,128)S(1)} %copy-done.2, ...), custom_call_target="tpu_custom_call" | custom-call | tf_op jit(solution)/shard_map/pallas_call | solution.py:279
  69.7 0.0 copy-start.1
  69.7 26.0 %all_to_all.20 = f32[512,1,128]{2,1,0:T(1,128)S(1)} all-to-all(f32[512,1,128]{2,1,0:T(1,128)S(1)} %bitcast.15), channel_id=1, replica_groups=mesh['row_0'=8,'row_1'=2,'row_2'=2,'col'=16] {'row_0','row_1','row_2','c..., dimensions={0} | all-to-all | bytes 524288 | tf_op jit(solution)/shard_map/all_to_all | solution.py:322
  95.7 1.2 %shard_map.133 = f32[16,16,256]{2,1,0:T(8,128)S(1)} custom-call(f32[1]{0:T(128)} %constant.136.clone.1, f32[512,128]{1,0:T(8,128)S(1)} %bitcast.14, f32[16,256]{1,0:T(8,128)S(1)} %copy-done.9, f32[16,256]{1,0:T(8,128)S(1)} %copy-done.8, f32[256,512]{1,0:T(8,128)S(1)} %copy-done.1), custom_call_target="tpu_custom_call" | custom-call | tf_op jit(solution)/shard_map/pallas_call | solution.py:279
  96.9 14.9 %all_to_all.21 = f32[16,16,256]{2,1,0:T(8,128)S(1)} all-to-all(f32[16,16,256]{2,1,0:T(8,128)S(1)} %shard_map.133), channel_id=1, replica_groups=mesh['row_0'=8,'row_1'=2,'row_2'=2,'col'=16] {'col'}, dimensions={0} | all-to-all | bytes 524288 | tf_op jit(solution)/shard_map/all_to_all | solution.py:326
  111.8 0.7 slice_bitcast_fusion
  (16 shorter events, 0.1 us)
Async XLA Ops:
  0.6 24.2 %copy-start = (f32[264,512]{1,0:T(8,128)S(1)}, f32[264,512]{1,0:T(8,128)}, u32[]{:S(2)}) copy-start(f32[264,512]{1,0:T(8,128)} %constant.170.clone.matrix) | copy-start | bytes 1622020
  2.4 22.4 %copy-start.9 = (f32[16,256]{1,0:T(8,128)S(1)}, f32[16,256]{1,0:T(8,128)}, u32[]{:S(2)}) copy-start(f32[16,256]{1,0:T(8,128)} %constant.168.clone.cos_y.rest_0_) | copy-start | bytes 49156
  2.4 22.4 %all-to-all-start = ((f32[16,16,256]{2,1,0:T(8,128)}), f32[16,16,256]{2,1,0:T(8,128)S(1)}, u32[]{:S(2)}, u32[]{:S(2)}) async-start(f32[16,16,256]{2,1,0:T(8,128)} %pad_maximum_fusion), calls=%async_computation | async-start | bytes 524288 | tf_op jit(solution)/shard_map/all_to_all | solution.py:303
  12.7 12.1 %copy-start.8 = (f32[16,256]{1,0:T(8,128)S(1)}, f32[16,256]{1,0:T(8,128)}, u32[]{:S(2)}) copy-start(f32[16,256]{1,0:T(8,128)} %constant.169.clone.sin_y.rest_1_) | copy-start | bytes 49156
  24.8 41.6 %copy-start.7 = (f32[512,128]{1,0:T(8,128)S(1)}, f32[512,128]{1,0:T(8,128)}, u32[]{:S(2)}) copy-start(f32[512,128]{1,0:T(8,128)} %constant.171.clone.cos_c) | copy-start | bytes 786436
  28.0 38.5 %copy-start.3 = (f32[256,256]{1,0:T(8,128)S(1)}, f32[256,256]{1,0:T(8,128)}, u32[]{:S(2)}) copy-start(f32[256,256]{1,0:T(8,128)} %constant.176.clone.backward) | copy-start | bytes 786436
  28.0 38.5 %copy-start.4 = (f32[512,128]{1,0:T(8,128)S(1)}, f32[512,128]{1,0:T(8,128)}, u32[]{:S(2)}) copy-start(f32[512,128]{1,0:T(8,128)} %constant.174.clone.sin_i) | copy-start | bytes 786436
  28.0 38.5 %copy-start.5 = (f32[512,128]{1,0:T(8,128)S(1)}, f32[512,128]{1,0:T(8,128)}, u32[]{:S(2)}) copy-start(f32[512,128]{1,0:T(8,128)} %constant.173.clone.cos_i) | copy-start | bytes 786436
  28.0 38.5 %copy-start.6 = (f32[512,128]{1,0:T(8,128)S(1)}, f32[512,128]{1,0:T(8,128)}, u32[]{:S(2)}) copy-start(f32[512,128]{1,0:T(8,128)} %constant.172.clone.sin_c) | copy-start | bytes 786436
  28.0 38.5 %all-to-all-start.1 = ((f32[512,2,128]{2,1,0:T(2,128)}), f32[512,2,128]{2,1,0:T(2,128)S(1)}, u32[]{:S(2)}, u32[]{:S(2)}) async-start(f32[512,2,128]{2,1,0:T(2,128)} %bitcast.3), calls=%async_computation.1 | async-start | bytes 1048576 | tf_op jit(solution)/shard_map/all_to_all | solution.py:305
  44.0 22.4 %copy-start.2 = (f32[256,512]{1,0:T(8,128)S(1)}, f32[256,512]{1,0:T(8,128)}, u32[]{:S(2)}) copy-start(f32[256,512]{1,0:T(8,128)} %constant.175.clone.forward) | copy-start | bytes 1572868
  69.7 26.0 %copy-start.1 = (f32[256,512]{1,0:T(8,128)S(1)}, f32[256,512]{1,0:T(8,128)}, u32[]{:S(2)}) copy-start(f32[256,512]{1,0:T(8,128)} %constant.177.clone.rest_2_) | copy-start | bytes 1572868

commit v2 on v1

--- a/solution.py
+++ b/solution.py
@@ -78,17 +78,23 @@
     return low + high[: n // 4][::-1]
 
 
+def halves(a):
+    high = a.astype(jnp.bfloat16)
+    return high, (a - high.astype(jnp.float32)).astype(jnp.bfloat16)
+
+
 def dot(a, b, dims=((1,), (0,))):
-    return lax.dot_general(
-        a, b, (dims, ((), ())), precision=lax.Precision.HIGHEST, preferred_element_type=jnp.float32
-    )
+    def product(u, v):
+        return lax.dot_general(u, v, (dims, ((), ())), preferred_element_type=jnp.float32)
+
+    return product(a[0], b[0]) + (product(a[1], b[0]) + product(a[0], b[1]))
 
 
 def lane_of(shape):
     return lax.broadcasted_iota(jnp.int32, shape, len(shape) - 1)
 
 
-def y_forward(fields, cos_y, sin_y, matrix, out, turned):
+def y_forward(fields, cos_y, sin_y, high, low, out, turned):
     for f in range(3):
         lines = []
         for c in range(C):
@@ -118,7 +124,7 @@
         turned[row : row + I, :] = jnp.zeros((I, 2 * M), jnp.float32)
     lane = lane_of((R, LANES))
     for t in range(4):
-        half = dot(matrix[...], turned[t * LANES : (t + 1) * LANES, :], ((1,), (1,)))
+        half = dot((high[...], low[...]), halves(turned[t * LANES : (t + 1) * LANES, :]), ((1,), (1,)))
         for part in range(2):
             blocks = [half[part * 128 + 32 * s : part * 128 + 32 * (s + 1), :] for s in range(4)]
             if t == 0 and part == 1:
@@ -132,7 +138,7 @@
                 out[pl.ds((4 * t + j) * 2 + part, R, stride=2 * C), :] = piece
 
 
-def x_section(first, lines, cos_c, sin_c, cos_i, sin_i, forward, backward, growth, forcing, out, a_re, a_im, wide):
+def x_section(place, lines, cos_c, sin_c, cos_r, sin_r, cos_k, sin_k, fh, fl, bh, bl, out, a_re, a_im, cos_i, sin_i, wide):
     for h in range(2):
         values = [
             (
@@ -153,14 +159,21 @@
             values.append((re * u + im * v, im * u - re * v))
         for k, (re, im) in enumerate(dft(values, -1)):
             rows = slice(k * R + 8 * h, k * R + 8 * h + 8)
-            u, v = cos_i[rows, :], sin_i[rows, :]
+            u, v = cos_r[8 * h : 8 * h + 8, :], sin_r[8 * h : 8 * h + 8, :]
+            if k:
+                c, d = cos_k[k : k + 1, :], sin_k[k : k + 1, :]
+                u, v = u * c - v * d, u * d + v * c
+            cos_i[rows, :], sin_i[rows, :] = u, v
             wide[rows, :LANES] = re * u + im * v
             wide[rows, LANES:] = im * u - re * v
-    spectra = dot(wide[...], forward[...])
-    g, f = growth[...], forcing[...]
-    wide[:, :LANES] = g * spectra[:, :LANES] + f * spectra[:, 2 * LANES : 3 * LANES]
-    wide[:, LANES:] = g * spectra[:, LANES : 2 * LANES] + f * spectra[:, 3 * LANES :]
-    wide[...] = dot(wide[...], backward[...])
+    for t in range(4):
+        rows = slice(t * LANES, (t + 1) * LANES)
+        spectra = dot(halves(wide[rows, :]), (fh[...], fl[...]))
+        g, f = factors(place, t * LANES)
+        re = g * spectra[:, :LANES] + f * spectra[:, 2 * LANES : 3 * LANES]
+        im = g * spectra[:, LANES : 2 * LANES] + f * spectra[:, 3 * LANES :]
+        advanced = halves(jnp.concatenate([re, im], axis=1))
+        wide[rows, :] = dot(advanced, (bh[...], bl[...]))
     for h in range(4):
         values = []
         for k in range(C):
@@ -174,7 +187,7 @@
             a_re[pl.ds(8 * h * C + c, 8, stride=C), :] = re * u - im * v
             a_im[pl.ds(8 * h * C + c, 8, stride=C), :] = im * u + re * v
     lane = lane_of((8, LANES))
-    packed = (lane < 80) & (first[0] == 1)
+    packed = (lane < 80) & (place[0] + place[1] == 0)
     for h in range(2):
         values = [
             (a_re[k * C + 8 * h : k * C + 8 * h + 8, :], a_im[k * C + 8 * h : k * C + 8 * h + 8, :])
@@ -185,7 +198,7 @@
             out[r * C + 8 * h : r * C + 8 * h + 8, :] = jnp.where(lane < 64, re, im)
 
 
-def y_backward(pieces, constant, cos_y, sin_y, matrix, out, spectrum, turned):
+def y_backward(pieces, cos_y, sin_y, high, low, out, spectrum, turned):
     lane = lane_of((R, LANES))
     for t in range(2):
         sources = [pieces[pl.ds(8 * t + j, R, stride=C), :] for j in range(8)]
@@ -196,7 +209,7 @@
                 block = moved if block is None else jnp.where(lane >= 16 * j, moved, block)
             spectrum[b * R : (b + 1) * R, t * LANES : (t + 1) * LANES] = block
     flipped = spectrum[...].T
-    turned[...] = dot(flipped, matrix[...])
+    turned[...] = dot(halves(flipped), (high[...], low[...]))
     parity = 1.0 - 2.0 * (lane_of((16, M)) % 2).astype(jnp.float32)
     values = []
     for k in range(C):
@@ -208,7 +221,8 @@
             re, im = re * u - im * v, im * u + re * v
         values.append((re, im))
     substrate_row = lax.broadcasted_iota(jnp.int32, (16, M), 0) < I
-    shift = jnp.where(substrate_row, constant[0], 0.0)
+    constant = math.expm1(-0.5 * FEED_RATE * TIME_STEP) / -FEED_RATE * FEED_RATE
+    shift = jnp.where(substrate_row, constant, 0.0)
     for c, (re, _) in enumerate(dft(values, 1)):
         out[c] = re + shift
 
@@ -228,8 +242,11 @@
     ones = np.ones((1, LANES))
     angle = 2 * np.pi / D * (outer * k_r % D)[:, None] * ones
     cos_c, sin_c = np.cos(angle), np.sin(angle)
-    angle = 2 * np.pi / N * ((k_r + R * outer)[:, None] * (np.arange(LANES) % I)[None, :] % N)
-    cos_i, sin_i = np.cos(angle), np.sin(angle)
+    lane_i = (np.arange(LANES) % I)[None, :]
+    angle = 2 * np.pi / N * (np.arange(R)[:, None] * lane_i)
+    cos_r, sin_r = np.cos(angle), np.sin(angle)
+    angle = 2 * np.pi / 128 * (np.arange(C)[:, None] * lane_i % 128)
+    cos_k, sin_k = np.cos(angle), np.sin(angle)
     angle = 2 * np.pi / I * (np.arange(I)[:, None] * np.arange(I)[None, :] % I)
     c, s = np.cos(angle), np.sin(angle)
     forward = np.zeros((2, LANES, 2, 2, LANES))
@@ -246,8 +263,17 @@
                 forward[0, there, kind, 1, here], forward[1, there, kind, 1, here] = -s, c
     forward = forward.reshape(2 * LANES, 4 * LANES)
     backward = backward.reshape(2 * LANES, 2 * LANES)
-    both = (cos_y, sin_y, y_matrix, y_inverse, cos_c, sin_c, cos_i, sin_i, forward, backward)
-    return [a.astype(f32) for a in both]
+    def parts(matrix):
+        high = matrix.astype(np.float32).astype(jnp.bfloat16)
+        return high, (matrix - high.astype(np.float64)).astype(jnp.bfloat16)
+
+    along_y = [a.astype(f32) for a in (cos_y, sin_y)]
+    along_x = [a.astype(f32) for a in (cos_c, sin_c, cos_r, sin_r, cos_k, sin_k)]
+    return (
+        (*along_y, *parts(y_matrix)),
+        (*along_x, *parts(forward), *parts(backward)),
+        (*along_y, *parts(y_inverse)),
+    )
 
 
 def signed_squares(wave_index):
@@ -256,22 +282,20 @@
     return angular * angular
 
 
-def factors(row_index, col_index):
-    row = lax.broadcasted_iota(jnp.int32, (D, LANES), 0)
-    lane = lane_of((D, LANES))
-    p = row % R + R * (row // R) + D * (lane % I)
-    slot = lane // 16
-    q = jnp.where(slot == 4, N // 2, col_index + C * (R * (slot % 4) + row_index))
+def factors(place, start):
+    row = start + lax.broadcasted_iota(jnp.int32, (LANES, LANES), 0)
+    lane = lane_of((1, LANES))
+    p = row + D * (lane & (I - 1))
+    slot = lane >> 4
+    q = jnp.where(slot == 4, N // 2, place[1] + C * (R * (slot & 3) + place[0]))
     wave_number = signed_squares(p) + signed_squares(q)
-    substrate = lane // I % 2 == 0
+    substrate = (lane & I) == 0
     diffusion = jnp.where(substrate, SUBSTRATE_DIFFUSION, ACTIVATOR_DIFFUSION)
     decay = jnp.where(substrate, FEED_RATE, FEED_RATE + KILL_RATE)
     linear = -diffusion * wave_number - decay
-    exponent = linear * (0.5 * TIME_STEP)
+    grown = jnp.exp(linear * (0.5 * TIME_STEP))
     normalize = 1.0 / (N * N)
-    growth = jnp.exp(exponent) * normalize
-    forcing = jnp.expm1(exponent) / linear * jnp.where(substrate, -normalize, normalize)
-    return growth, forcing
+    return grown * normalize, (grown - 1.0) / linear * jnp.where(substrate, -normalize, normalize)
 
 
 def call(body, out_shape, scratch, *operands, scalars=0):
@@ -286,43 +310,18 @@
     )(*operands)
 
 
-def y_backward_body(constant, pieces, *rest):
-    return y_backward(pieces, constant, *rest)
-
-
 def on_device(substrate, activator):
-    cos_y, sin_y, y_matrix, y_inverse, cos_c, sin_c, cos_i, sin_i, forward, backward = tables()
-    row_index = lax.axis_index(ROW)
-    col_index = lax.axis_index("col")
-    growth, forcing = factors(row_index, col_index)
-    first = ((row_index == 0) & (col_index == 0)).astype(jnp.int32).reshape(1)
-    rate = jnp.full((1,), -FEED_RATE, jnp.float32)
-    constant = jnp.expm1(rate * (0.5 * TIME_STEP)) / rate * FEED_RATE
-
+    along_y, along_x, back_y = tables()
+    place = jnp.stack([lax.axis_index(ROW), lax.axis_index("col")])
     fields = jnp.concatenate([substrate.reshape(C, I, M), activator.reshape(C, I, M)], axis=1)
+    fields, place = lax.optimization_barrier((fields, place))
     fields = lax.all_to_all(fields, "col", 0, 0, tiled=True)
-    pieces = call(y_forward, (2 * D, LANES), [(512, 2 * M)], fields, cos_y, sin_y, y_matrix)
+    pieces = call(y_forward, (2 * D, LANES), [(D, 2 * M)], fields, *along_y)
     lines = lax.all_to_all(pieces.reshape(D, 2, LANES), ALL, 0, 0, tiled=True).reshape(2 * D, LANES)
-    pieces = call(
-        x_section,
-        (D, LANES),
-        [(D, LANES), (D, LANES), (D, 2 * LANES)],
-        first,
-        lines,
-        cos_c,
-        sin_c,
-        cos_i,
-        sin_i,
-        forward,
-        backward,
-        growth,
-        forcing,
-        scalars=1,
-    )
+    scratch = [(D, LANES)] * 4 + [(D, 2 * LANES)]
+    pieces = call(x_section, (D, LANES), scratch, place, lines, *along_x, scalars=1)
     pieces = lax.all_to_all(pieces.reshape(D, 1, LANES), ALL, 0, 0, tiled=True).reshape(D, LANES)
-    fields = call(
-        y_backward_body, (C, 2 * I, M), [(M, M), (M, 2 * M)], constant, pieces, cos_y, sin_y, y_inverse, scalars=1
-    )
+    fields = call(y_backward, (C, 2 * I, M), [(M, M), (M, 2 * M)], pieces, *back_y)
     fields = lax.all_to_all(fields, "col", 0, 0, tiled=True)
     return (fields[:, :I].reshape(C * I, M), fields[:, I:].reshape(C * I, M))
 

time: 113 us -> 110 us (0.973)
  blocking collectives: 40.9 us -> 101 us
  waiting for transfers between devices: 33.8 us -> 0 us
  starting transfers between devices: 26.4 us -> 0 us
  Pallas kernels: 7.53 us -> 5.27 us
  other arithmetic: 2.29 us -> 1.1 us
    all_to_all x0 -> x1, blocking collectives: none -> 38.2 us  [on_device(): lax.all_to_all(pieces.reshape(D, 2, LANES), ALL, 0, 0, tiled=True)]
    all_to_all x2 -> x0, waiting for transfers between devices: 33.8 us -> none  [the longest x1 21.8 us: on_device(): lax.all_to_all(pieces.reshape(D, 2, LANES), ALL, 0, 0, tiled=True)]
    all_to_all x2 -> x0, starting transfers between devices: 26.4 us -> none  [the longest x1 16 us: on_device(): lax.all_to_all(pieces.reshape(D, 2, LANES), ALL, 0, 0, tiled=True)]
    all_to_all x1 -> x2, blocking collectives: 14.9 us -> 37.1 us  [on_device(): fields = lax.all_to_all(fields, 'col', 0, 0, tiled=True)]
    pallas_call x3, Pallas kernels: 7.53 us -> 5.27 us  [call(): pl.pallas_call(body, out_shape=jax.ShapeDtypeStruct(out_shape, jnp.float3...]
  transfers between devices with their start and end apart: 2 -> 0, of which waited for: 2 -> 0; matrix products, arithmetic and copies ran while one was open for 0% -> 0% of each run, Pallas kernels for 0% -> 0%
where the time goes in v2:
time: 110 us; the launch traced here: 109 us
  blocking collectives  101 us (92%)
  Pallas kernels  5.27 us (5%)
  other arithmetic  1.1 us (1%)
    all_to_all x1, blocking collectives, on_device(): lax.all_to_all(pieces.reshape(D, 2, LANES), ALL, 0, 0, tiled=True)  38.2 us
    all_to_all x2, blocking collectives, on_device(): fields = lax.all_to_all(fields, 'col', 0, 0, tiled=True)  37.1 us
    all_to_all x1, blocking collectives, on_device(): lax.all_to_all(pieces.reshape(D, 1, LANES), ALL, 0, 0, tiled=True)  26.1 us
    pallas_call x3, Pallas kernels, call(): pl.pallas_call(body, out_shape=jax.ShapeDtypeStruct(out_shape, jnp.float3...  5.27 us

profile of v2, /device:TPU:1, one launch (start us, length us, event | category | flops | bytes accessed | tf_op | source)
XLA Modules:
  0.0 109.5 jit_solution(287034642074791636)
XLA Ops:
  0.6 0.1 pad_add_fusion.place
  0.7 1.0 pad_maximum_fusion
  1.7 0.0 copy-start
  1.8 0.0 copy-start.10
  1.8 0.0 copy-start.11
  1.8 22.2 %all_to_all.20.fields = f32[16,16,256]{2,1,0:T(8,128)S(1)} all-to-all(f32[16,16,256]{2,1,0:T(8,128)S(1)} %pad_maximum_fusion), channel_id=1, replica_groups=mesh['row_0'=8,'row_1'=2,'row_2'=2,'col'=16] {'col'}, dimensions={0} | all-to-all | bytes 524288 | tf_op jit(solution)/shard_map/all_to_all | solution.py:318
  24.0 0.0 copy-start.8
  24.0 0.0 copy-start.9
  24.0 0.0 copy-start.12
  24.1 0.0 copy-start.13
  24.1 0.0 copy-start.14
  24.1 0.0 copy-start.15
  24.1 1.6 %shard_map.185 = f32[1024,128]{1,0:T(8,128)S(1)} custom-call(f32[16,16,256]{2,1,0:T(8,128)S(1)} %all_to_all.20.fields, f32[16,256]{1,0:T(8,128)S(1)} %copy-done.11, f32[16,256]{1,0:T(8,128)S(1)} %copy-done.10, bf16[264,512]{1,0:T(8,128)(2,1)S(1)} %copy-done.1, bf16[264,512]{1,0:T(8,128)(2,1)S(1)} %copy-done), custom_call_target="tpu_custom_call" | custom-call | tf_op jit(solution)/shard_map/pallas_call | solution.py:303
  25.7 0.0 copy-start.2
  25.7 0.0 copy-start.3
  25.7 0.0 copy-start.4
  25.7 0.0 copy-start.5
  25.7 38.2 %all_to_all.21 = f32[512,2,128]{2,1,0:T(2,128)S(1)} all-to-all(f32[512,2,128]{2,1,0:T(2,128)S(1)} %bitcast.15), channel_id=1, replica_groups=mesh['row_0'=8,'row_1'=2,'row_2'=2,'col'=16] {'row_0','row_1','row_2','c..., dimensions={0} | all-to-all | bytes 1048576 | tf_op jit(solution)/shard_map/all_to_all | solution.py:320
  64.1 2.7 %shard_map.186 = f32[512,128]{1,0:T(8,128)S(1)} custom-call(s32[2]{0:T(128)S(1)} %pad_add_fusion.place, f32[1024,128]{1,0:T(8,128)S(1)} %bitcast.14, f32[512,128]{1,0:T(8,128)S(1)} %copy-done.5, f32[512,128]{1,0:T(8,128)S(1)} %copy-done.4, f32[32,128]{1,0:T(8,128)S(1)} %copy-done.13, f32[32,128]{1,0:T(8,128)S(1)} %copy-done.12, f32[16,128]{1,0:T(8,128)S(1)} %copy-done.15, ...), custom_call_target="tpu_custom_call" | custom-call | tf_op jit(solution)/shard_map/pallas_call | solution.py:303
  66.7 0.0 copy-start.7
  66.8 26.1 %all_to_all.22 = f32[512,1,128]{2,1,0:T(1,128)S(1)} all-to-all(f32[512,1,128]{2,1,0:T(1,128)S(1)} %bitcast.16), channel_id=1, replica_groups=mesh['row_0'=8,'row_1'=2,'row_2'=2,'col'=16] {'row_0','row_1','row_2','c..., dimensions={0} | all-to-all | bytes 524288 | tf_op jit(solution)/shard_map/all_to_all | solution.py:323
  92.8 1.0 shard_map.187
  93.9 14.9 %all_to_all.23 = f32[16,16,256]{2,1,0:T(8,128)S(1)} all-to-all(f32[16,16,256]{2,1,0:T(8,128)S(1)} %shard_map.187), channel_id=1, replica_groups=mesh['row_0'=8,'row_1'=2,'row_2'=2,'col'=16] {'col'}, dimensions={0} | all-to-all | bytes 524288 | tf_op jit(solution)/shard_map/all_to_all | solution.py:325
  108.7 0.7 slice_bitcast_fusion
  (18 shorter events, 0.0 us)
Async XLA Ops:
  0.7 23.3 %copy-start.1 = (bf16[264,512]{1,0:T(8,128)(2,1)S(1)}, bf16[264,512]{1,0:T(8,128)(2,1)}, u32[]{:S(2)}) copy-start(bf16[264,512]{1,0:T(8,128)(2,1)} %constant.57.clone.high) | copy-start | bytes 811012
  1.7 22.3 %copy-start = (bf16[264,512]{1,0:T(8,128)(2,1)S(1)}, bf16[264,512]{1,0:T(8,128)(2,1)}, u32[]{:S(2)}) copy-start(bf16[264,512]{1,0:T(8,128)(2,1)} %constant.58.clone.low) | copy-start | bytes 811012
  1.8 22.2 %copy-start.10 = (f32[16,256]{1,0:T(8,128)S(1)}, f32[16,256]{1,0:T(8,128)}, u32[]{:S(2)}) copy-start(f32[16,256]{1,0:T(8,128)} %constant.56.clone.sin_y) | copy-start | bytes 49156
  1.8 22.2 %copy-start.11 = (f32[16,256]{1,0:T(8,128)S(1)}, f32[16,256]{1,0:T(8,128)}, u32[]{:S(2)}) copy-start(f32[16,256]{1,0:T(8,128)} %constant.55.clone.cos_y) | copy-start | bytes 49156
  24.0 40.0 %copy-start.8 = (bf16[256,256]{1,0:T(8,128)(2,1)S(1)}, bf16[256,256]{1,0:T(8,128)(2,1)}, u32[]{:S(2)}) copy-start(bf16[256,256]{1,0:T(8,128)(2,1)} %constant.68.clone.bl) | copy-start | bytes 393220
  24.0 40.0 %copy-start.9 = (bf16[256,256]{1,0:T(8,128)(2,1)S(1)}, bf16[256,256]{1,0:T(8,128)(2,1)}, u32[]{:S(2)}) copy-start(bf16[256,256]{1,0:T(8,128)(2,1)} %constant.67.clone.bh) | copy-start | bytes 393220
  24.0 40.0 %copy-start.12 = (f32[32,128]{1,0:T(8,128)S(1)}, f32[32,128]{1,0:T(8,128)}, u32[]{:S(2)}) copy-start(f32[32,128]{1,0:T(8,128)} %constant.62.clone.sin_r) | copy-start | bytes 49156
  24.1 40.0 %copy-start.13 = (f32[32,128]{1,0:T(8,128)S(1)}, f32[32,128]{1,0:T(8,128)}, u32[]{:S(2)}) copy-start(f32[32,128]{1,0:T(8,128)} %constant.61.clone.cos_r) | copy-start | bytes 49156
  24.1 39.9 %copy-start.14 = (f32[16,128]{1,0:T(8,128)S(1)}, f32[16,128]{1,0:T(8,128)}, u32[]{:S(2)}) copy-start(f32[16,128]{1,0:T(8,128)} %constant.64.clone.sin_k) | copy-start | bytes 24580
  24.1 39.9 %copy-start.15 = (f32[16,128]{1,0:T(8,128)S(1)}, f32[16,128]{1,0:T(8,128)}, u32[]{:S(2)}) copy-start(f32[16,128]{1,0:T(8,128)} %constant.63.clone.cos_k) | copy-start | bytes 24580
  25.7 38.3 %copy-start.2 = (bf16[256,512]{1,0:T(8,128)(2,1)S(1)}, bf16[256,512]{1,0:T(8,128)(2,1)}, u32[]{:S(2)}) copy-start(bf16[256,512]{1,0:T(8,128)(2,1)} %constant.66.clone.fl) | copy-start | bytes 786436
  25.7 38.3 %copy-start.3 = (bf16[256,512]{1,0:T(8,128)(2,1)S(1)}, bf16[256,512]{1,0:T(8,128)(2,1)}, u32[]{:S(2)}) copy-start(bf16[256,512]{1,0:T(8,128)(2,1)} %constant.65.clone.fh) | copy-start | bytes 786436
  25.7 38.3 %copy-start.4 = (f32[512,128]{1,0:T(8,128)S(1)}, f32[512,128]{1,0:T(8,128)}, u32[]{:S(2)}) copy-start(f32[512,128]{1,0:T(8,128)} %constant.60.clone.sin_c) | copy-start | bytes 786436
  25.7 38.3 %copy-start.5 = (f32[512,128]{1,0:T(8,128)S(1)}, f32[512,128]{1,0:T(8,128)}, u32[]{:S(2)}) copy-start(f32[512,128]{1,0:T(8,128)} %constant.59.clone.cos_c) | copy-start | bytes 786436
  66.7 26.1 %copy-start.6 = (bf16[256,512]{1,0:T(8,128)(2,1)S(1)}, bf16[256,512]{1,0:T(8,128)(2,1)}, u32[]{:S(2)}) copy-start(bf16[256,512]{1,0:T(8,128)(2,1)} %constant.70.clone.low) | copy-start | bytes 786436
  66.7 26.1 %copy-start.7 = (bf16[256,512]{1,0:T(8,128)(2,1)S(1)}, bf16[256,512]{1,0:T(8,128)(2,1)}, u32[]{:S(2)}) copy-start(bf16[256,512]{1,0:T(8,128)(2,1)} %constant.69.clone.high) | copy-start | bytes 786436

commit v3 on v2

--- a/solution.py
+++ b/solution.py
@@ -92,6 +92,13 @@
 
 def lane_of(shape):
     return lax.broadcasted_iota(jnp.int32, shape, len(shape) - 1)
+
+
+def by_block(sources, width, lane):
+    piece = sources[0]
+    for k, source in enumerate(sources[1:], 1):
+        piece = jnp.where(lane >= width * k, source, piece)
+    return piece
 
 
 def y_forward(fields, cos_y, sin_y, high, low, out, turned):
@@ -122,80 +129,103 @@
     for k in range(C):
         row = k * 32 + 3 * I
         turned[row : row + I, :] = jnp.zeros((I, 2 * M), jnp.float32)
+    parity = 1.0 - 2.0 * (lane_of((I, M)) & 1).astype(jnp.float32)
+    place = lane_of((I, LANES))
+    last = jnp.zeros((I, LANES), jnp.float32)
+    for f in range(3):
+        total = jnp.sum(turned[f * I : (f + 1) * I, :M] * parity, axis=1, keepdims=True)
+        last = jnp.where(place == 32 * f, total, last)
     lane = lane_of((R, LANES))
     for t in range(4):
-        half = dot((high[...], low[...]), halves(turned[t * LANES : (t + 1) * LANES, :]), ((1,), (1,)))
+        spectra = dot(halves(turned[t * LANES : (t + 1) * LANES, :]), (high[...], low[...]))
         for part in range(2):
-            blocks = [half[part * 128 + 32 * s : part * 128 + 32 * (s + 1), :] for s in range(4)]
-            if t == 0 and part == 1:
-                first = (lax.broadcasted_iota(jnp.int32, (R, LANES), 0) == 0) & (lane < 32)
-                blocks[0] = jnp.where(first, half[256:257, :], blocks[0])
+            half = spectra[:, part * LANES : (part + 1) * LANES]
+            if t == 0 and part == 0:
+                half = jnp.concatenate([half[: 3 * I], last, half[4 * I :]], axis=0)
+            half = half.T
+            blocks = [half[32 * s : 32 * (s + 1), :] for s in range(4)]
+            blocks = [blocks[0]] + [pltpu.roll(blocks[s], 32 * s, 1) for s in range(1, 4)]
             for j in range(4):
-                piece = None
-                for s in range(4):
-                    moved = blocks[s] if s == j else pltpu.roll(blocks[s], 32 * (s - j) % LANES, 1)
-                    piece = moved if piece is None else jnp.where(lane >= 32 * s, moved, piece)
+                piece = by_block([blocks[(k - j) % 4] for k in range(4)], 32, lane)
                 out[pl.ds((4 * t + j) * 2 + part, R, stride=2 * C), :] = piece
 
 
-def x_section(place, lines, cos_c, sin_c, cos_r, sin_r, cos_k, sin_k, fh, fl, bh, bl, out, a_re, a_im, cos_i, sin_i, wide):
+def swapped(z):
+    return pltpu.roll(z, 64, 1)
+
+
+def packed_dft(values, signs):
+    n = len(values)
+    if n == 1:
+        return values
+    even, odd = packed_dft(values[0::2], signs), packed_dft(values[1::2], signs)
+    for k in range(1, n // 2):
+        c, s = unit(k, n, 1)
+        turned = swapped(odd[k]) * (signs if s == 1.0 else signs * s)
+        odd[k] = turned if c == 0.0 else odd[k] * c + turned
+    return [e + o for e, o in zip(even, odd)] + [e - o for e, o in zip(even, odd)]
+
+
+def x_section(
+    place, lines, cos_c, sin_c, cos_r, sin_r, cos_k, sin_k, decay, fh, fl, bh, bl, out, a_re, a_im, cos_i, sin_i, wide
+):
+    back = (LANES - 32 * (place[1] & 3)) & (LANES - 1)
     for h in range(2):
         values = [
-            (
-                lines[pl.ds(32 * r + 16 * h, 8, stride=2), :],
-                lines[pl.ds(32 * r + 16 * h + 1, 8, stride=2), :],
+            tuple(
+                pltpu.roll(lines[pl.ds(32 * r + 16 * h + part, 8, stride=2), :], back, 1) for part in range(2)
             )
             for r in range(R)
         ]
         for k, (re, im) in enumerate(dft(values, -1)):
             a_re[k * C + 8 * h : k * C + 8 * h + 8, :] = re
             a_im[k * C + 8 * h : k * C + 8 * h + 8, :] = im
+    signs = jnp.where(lane_of((8, LANES)) < 64, -1.0, 1.0)
     for h in range(4):
         values = []
         for c in range(C):
             rows = slice(c * R + 8 * h, c * R + 8 * h + 8)
             re, im = a_re[pl.ds(8 * h * C + c, 8, stride=C), :], a_im[pl.ds(8 * h * C + c, 8, stride=C), :]
-            u, v = cos_c[rows, :], sin_c[rows, :]
-            values.append((re * u + im * v, im * u - re * v))
+            if c:
+                u, v = cos_c[rows, :], sin_c[rows, :]
+                re, im = re * u + im * v, im * u - re * v
+            values.append((re, im))
         for k, (re, im) in enumerate(dft(values, -1)):
             rows = slice(k * R + 8 * h, k * R + 8 * h + 8)
             u, v = cos_r[8 * h : 8 * h + 8, :], sin_r[8 * h : 8 * h + 8, :]
             if k:
                 c, d = cos_k[k : k + 1, :], sin_k[k : k + 1, :]
                 u, v = u * c - v * d, u * d + v * c
-            cos_i[rows, :], sin_i[rows, :] = u, v
+            cos_i[rows, :], sin_i[rows, :] = u, v * signs
             wide[rows, :LANES] = re * u + im * v
             wide[rows, LANES:] = im * u - re * v
+    along_y, normal = column_factors(place)
     for t in range(4):
         rows = slice(t * LANES, (t + 1) * LANES)
         spectra = dot(halves(wide[rows, :]), (fh[...], fl[...]))
-        g, f = factors(place, t * LANES)
+        linear = decay[rows, :] + along_y
+        grown = jnp.exp(linear * (0.5 * TIME_STEP))
+        g, f = grown * (1.0 / (N * N)), (grown - 1.0) / linear * normal
         re = g * spectra[:, :LANES] + f * spectra[:, 2 * LANES : 3 * LANES]
         im = g * spectra[:, LANES : 2 * LANES] + f * spectra[:, 3 * LANES :]
         advanced = halves(jnp.concatenate([re, im], axis=1))
-        wide[rows, :] = dot(advanced, (bh[...], bl[...]))
+        wide[rows, :LANES] = dot(advanced, (bh[...], bl[...]))
     for h in range(4):
         values = []
         for k in range(C):
             rows = slice(k * R + 8 * h, k * R + 8 * h + 8)
-            re, im = wide[rows, :LANES], wide[rows, LANES:]
-            u, v = cos_i[rows, :], sin_i[rows, :]
-            values.append((re * u - im * v, im * u + re * v))
-        for c, (re, im) in enumerate(dft(values, 1)):
+            z = wide[rows, :LANES]
+            values.append(z * cos_i[rows, :] + swapped(z) * sin_i[rows, :])
+        for c, z in enumerate(packed_dft(values, signs)):
             rows = slice(c * R + 8 * h, c * R + 8 * h + 8)
-            u, v = cos_c[rows, :], sin_c[rows, :]
-            a_re[pl.ds(8 * h * C + c, 8, stride=C), :] = re * u - im * v
-            a_im[pl.ds(8 * h * C + c, 8, stride=C), :] = im * u + re * v
-    lane = lane_of((8, LANES))
-    packed = (lane < 80) & (place[0] + place[1] == 0)
+            if c:
+                z = z * cos_c[rows, :] + swapped(z) * (sin_c[rows, :] * signs)
+            a_re[pl.ds(8 * h * C + c, 8, stride=C), :] = z
+    on = 16 * (place[1] & 7)
     for h in range(2):
-        values = [
-            (a_re[k * C + 8 * h : k * C + 8 * h + 8, :], a_im[k * C + 8 * h : k * C + 8 * h + 8, :])
-            for k in range(R)
-        ]
-        for r, (re, im) in enumerate(dft(values, 1)):
-            im = jnp.where(packed, im, pltpu.roll(im, 64, 1))
-            out[r * C + 8 * h : r * C + 8 * h + 8, :] = jnp.where(lane < 64, re, im)
+        values = [a_re[k * C + 8 * h : k * C + 8 * h + 8, :] for k in range(R)]
+        for r, z in enumerate(packed_dft(values, signs)):
+            out[r * C + 8 * h : r * C + 8 * h + 8, :] = pltpu.roll(z, on, 1)
 
 
 def y_backward(pieces, cos_y, sin_y, high, low, out, spectrum, turned):
@@ -203,14 +233,12 @@
     for t in range(2):
         sources = [pieces[pl.ds(8 * t + j, R, stride=C), :] for j in range(8)]
         for b in range(8):
-            block = None
-            for j in range(8):
-                moved = sources[j] if j == b else pltpu.roll(sources[j], 16 * (j - b) % LANES, 1)
-                block = moved if block is None else jnp.where(lane >= 16 * j, moved, block)
+            block = by_block([sources[(k - b) % 8] for k in range(8)], 16, lane)
+            block = pltpu.roll(block, LANES - 16 * b, 1) if b else block
             spectrum[b * R : (b + 1) * R, t * LANES : (t + 1) * LANES] = block
     flipped = spectrum[...].T
     turned[...] = dot(halves(flipped), (high[...], low[...]))
-    parity = 1.0 - 2.0 * (lane_of((16, M)) % 2).astype(jnp.float32)
+    parity = 1.0 - 2.0 * (lane_of((16, M)) & 1).astype(jnp.float32)
     values = []
     for k in range(C):
         re, im = turned[16 * k : 16 * (k + 1), :M], turned[16 * k : 16 * (k + 1), M:]
@@ -231,12 +259,10 @@
     f32 = np.float32
     angle = 2 * np.pi / N * (np.arange(C)[:, None] * np.arange(M)[None, :])
     cos_y, sin_y = np.cos(angle), np.sin(angle)
-    turn_m = 2 * np.pi / M * (np.arange(128)[:, None] * np.arange(M)[None, :] % M)
+    turn_m = 2 * np.pi / M * (np.arange(M)[:, None] * np.arange(128)[None, :] % M)
     c, s = np.cos(turn_m), np.sin(turn_m)
-    last = np.zeros((8, 2 * M))
-    last[0, :M] = 1 - 2 * (np.arange(M) % 2)
-    y_matrix = np.concatenate([np.block([[c, s], [-s, c]]), last])
-    y_inverse = 2 * np.block([[c, s], [-s, c]])
+    y_matrix = np.block([[c, -s], [s, c]])
+    y_inverse = 2 * np.block([[c.T, s.T], [-s.T, c.T]])
     k_r = np.tile(np.arange(R), C)
     outer = np.repeat(np.arange(C), R)
     ones = np.ones((1, LANES))
@@ -250,25 +276,37 @@
     angle = 2 * np.pi / I * (np.arange(I)[:, None] * np.arange(I)[None, :] % I)
     c, s = np.cos(angle), np.sin(angle)
     forward = np.zeros((2, LANES, 2, 2, LANES))
-    backward = np.zeros((2, LANES, 2, LANES))
+    backward = np.zeros((2, LANES, LANES))
     for slot in range(5):
         for field in range(2):
             here = slice(16 * slot + I * field, 16 * slot + I * field + I)
-            backward[0, here, 0, here], backward[1, here, 0, here] = c, -s
-            backward[0, here, 1, here], backward[1, here, 1, here] = s, c
+            if slot < 4:
+                there = slice(64 + here.start, 64 + here.stop)
+                backward[0, here, here], backward[1, here, here] = c, -s
+                backward[0, here, there], backward[1, here, there] = s, c
+            else:
+                start = slice(I * field, I * field + I)
+                there = slice(64 + I * field, 64 + I * field + I)
+                backward[0, here, start], backward[1, here, start] = -s, -c
+                backward[0, here, there], backward[1, here, there] = c, -s
             for kind, taken in enumerate((field, 2)):
-                start = 32 * (slot % 4) + I * taken
+                start = 32 * slot + I * taken if slot < 4 else 32 * taken + 3 * I
                 there = slice(start, start + I)
                 forward[0, there, kind, 0, here], forward[1, there, kind, 0, here] = c, s
                 forward[0, there, kind, 1, here], forward[1, there, kind, 1, here] = -s, c
     forward = forward.reshape(2 * LANES, 4 * LANES)
-    backward = backward.reshape(2 * LANES, 2 * LANES)
+    backward = backward.reshape(2 * LANES, LANES)
+    lane = np.arange(LANES)[None, :]
+    p = np.arange(D)[:, None] + D * (lane % I)
+    angular = 2 * np.pi * np.where(2 * p < N, p, p - N)
+    decay = -np.where(lane // I % 2 == 0, SUBSTRATE_DIFFUSION, ACTIVATOR_DIFFUSION) * angular**2
+
     def parts(matrix):
         high = matrix.astype(np.float32).astype(jnp.bfloat16)
         return high, (matrix - high.astype(np.float64)).astype(jnp.bfloat16)
 
     along_y = [a.astype(f32) for a in (cos_y, sin_y)]
-    along_x = [a.astype(f32) for a in (cos_c, sin_c, cos_r, sin_r, cos_k, sin_k)]
+    along_x = [a.astype(f32) for a in (cos_c, sin_c, cos_r, sin_r, cos_k, sin_k, decay)]
     return (
         (*along_y, *parts(y_matrix)),
         (*along_x, *parts(forward), *parts(backward)),
@@ -276,26 +314,17 @@
     )
 
 
-def signed_squares(wave_index):
-    signed = jnp.where(2 * wave_index < N, wave_index, wave_index - N).astype(jnp.float32)
-    angular = 2.0 * math.pi * signed
-    return angular * angular
-
-
-def factors(place, start):
-    row = start + lax.broadcasted_iota(jnp.int32, (LANES, LANES), 0)
+def column_factors(place):
     lane = lane_of((1, LANES))
-    p = row + D * (lane & (I - 1))
     slot = lane >> 4
     q = jnp.where(slot == 4, N // 2, place[1] + C * (R * (slot & 3) + place[0]))
-    wave_number = signed_squares(p) + signed_squares(q)
+    signed = jnp.where(2 * q < N, q, q - N).astype(jnp.float32)
+    angular = 2.0 * math.pi * signed
     substrate = (lane & I) == 0
     diffusion = jnp.where(substrate, SUBSTRATE_DIFFUSION, ACTIVATOR_DIFFUSION)
     decay = jnp.where(substrate, FEED_RATE, FEED_RATE + KILL_RATE)
-    linear = -diffusion * wave_number - decay
-    grown = jnp.exp(linear * (0.5 * TIME_STEP))
     normalize = 1.0 / (N * N)
-    return grown * normalize, (grown - 1.0) / linear * jnp.where(substrate, -normalize, normalize)
+    return -diffusion * (angular * angular) - decay, jnp.where(substrate, -normalize, normalize)
 
 
 def call(body, out_shape, scratch, *operands, scalars=0):

time: 110 us -> 110 us (level)
  no operation moved by 1% of the time
where the time goes in v3:
time: 110 us; the launch traced here: 109 us
  blocking collectives  101 us (92%)
  Pallas kernels  4.98 us (5%)
    all_to_all x1, blocking collectives, on_device(): lax.all_to_all(pieces.reshape(D, 2, LANES), ALL, 0, 0, tiled=True)  38.3 us
    all_to_all x2, blocking collectives, on_device(): fields = lax.all_to_all(fields, 'col', 0, 0, tiled=True)  37.1 us
    all_to_all x1, blocking collectives, on_device(): lax.all_to_all(pieces.reshape(D, 1, LANES), ALL, 0, 0, tiled=True)  26.1 us
    pallas_call x3, Pallas kernels, call(): pl.pallas_call(body, out_shape=jax.ShapeDtypeStruct(out_shape, jnp.float3...  4.98 us

profile of v3, /device:TPU:1, one launch (start us, length us, event | category | flops | bytes accessed | tf_op | source)
XLA Modules:
  0.0 109.2 jit_solution(8068202781216098851)
XLA Ops:
  0.6 0.1 pad_add_fusion.place
  0.7 1.0 pad_maximum_fusion
  1.7 0.0 copy-start.7
  1.7 0.0 copy-start.8
  1.7 22.2 %all_to_all.20.fields = f32[16,16,256]{2,1,0:T(8,128)S(1)} all-to-all(f32[16,16,256]{2,1,0:T(8,128)S(1)} %pad_maximum_fusion), channel_id=1, replica_groups=mesh['row_0'=8,'row_1'=2,'row_2'=2,'col'=16] {'col'}, dimensions={0} | all-to-all | bytes 524288 | tf_op jit(solution)/shard_map/all_to_all | solution.py:347
  24.0 0.0 copy-start.4
  24.0 0.0 copy-start.11
  24.0 0.0 copy-start.12
  24.0 0.0 copy-start.13
  24.0 0.0 copy-start.14
  24.0 0.0 copy-start.15
  24.1 0.0 copy-start.16
  24.1 1.1 shard_map.194
  25.1 0.0 copy-start
  25.2 0.0 copy-start.1
  25.2 0.0 copy-start.2
  25.2 38.3 %all_to_all.21 = f32[512,2,128]{2,1,0:T(2,128)S(1)} all-to-all(f32[512,2,128]{2,1,0:T(2,128)S(1)} %bitcast.15), channel_id=1, replica_groups=mesh['row_0'=8,'row_1'=2,'row_2'=2,'col'=16] {'row_0','row_1','row_2','c..., dimensions={0} | all-to-all | bytes 1048576 | tf_op jit(solution)/shard_map/all_to_all | solution.py:349
  63.5 3.3 %shard_map.195 = f32[512,128]{1,0:T(8,128)S(1)} custom-call(s32[2]{0:T(128)S(1)} %pad_add_fusion.place, f32[1024,128]{1,0:T(8,128)S(1)} %bitcast.14, f32[512,128]{1,0:T(8,128)S(1)} %copy-done.4, f32[512,128]{1,0:T(8,128)S(1)} %copy-done.3, f32[32,128]{1,0:T(8,128)S(1)} %copy-done.14, f32[32,128]{1,0:T(8,128)S(1)} %copy-done.13, f32[16,128]{1,0:T(8,128)S(1)} %copy-done.16, ...), custom_call_target="tpu_custom_call" | custom-call | tf_op jit(solution)/shard_map/pallas_call | solution.py:332
  66.8 0.0 copy-start.5
  66.8 0.0 copy-start.6
  66.9 26.1 %all_to_all.22 = f32[512,1,128]{2,1,0:T(1,128)S(1)} all-to-all(f32[512,1,128]{2,1,0:T(1,128)S(1)} %bitcast.16), channel_id=1, replica_groups=mesh['row_0'=8,'row_1'=2,'row_2'=2,'col'=16] {'row_0','row_1','row_2','c..., dimensions={0} | all-to-all | bytes 524288 | tf_op jit(solution)/shard_map/all_to_all | solution.py:352
  92.9 0.6 shard_map.196
  93.6 14.9 %all_to_all.23 = f32[16,16,256]{2,1,0:T(8,128)S(1)} all-to-all(f32[16,16,256]{2,1,0:T(8,128)S(1)} %shard_map.196), channel_id=1, replica_groups=mesh['row_0'=8,'row_1'=2,'row_2'=2,'col'=16] {'col'}, dimensions={0} | all-to-all | bytes 524288 | tf_op jit(solution)/shard_map/all_to_all | solution.py:354
  108.4 0.7 slice_bitcast_fusion
  (20 shorter events, 0.0 us)
Async XLA Ops:
  0.7 23.2 %copy-start.9 = (f32[16,256]{1,0:T(8,128)S(1)}, f32[16,256]{1,0:T(8,128)}, u32[]{:S(2)}) copy-start(f32[16,256]{1,0:T(8,128)} %constant.58.clone.sin_y) | copy-start | bytes 49156
  0.7 23.3 %copy-start.10 = (f32[16,256]{1,0:T(8,128)S(1)}, f32[16,256]{1,0:T(8,128)}, u32[]{:S(2)}) copy-start(f32[16,256]{1,0:T(8,128)} %constant.57.clone.cos_y) | copy-start | bytes 49156
  1.7 22.2 %copy-start.7 = (bf16[512,256]{1,0:T(8,128)(2,1)S(1)}, bf16[512,256]{1,0:T(8,128)(2,1)}, u32[]{:S(2)}) copy-start(bf16[512,256]{1,0:T(8,128)(2,1)} %constant.60.clone.low) | copy-start | bytes 786436
  1.7 22.2 %copy-start.8 = (bf16[512,256]{1,0:T(8,128)(2,1)S(1)}, bf16[512,256]{1,0:T(8,128)(2,1)}, u32[]{:S(2)}) copy-start(bf16[512,256]{1,0:T(8,128)(2,1)} %constant.59.clone.high) | copy-start | bytes 786436
  24.0 39.5 %copy-start.4 = (f32[512,128]{1,0:T(8,128)S(1)}, f32[512,128]{1,0:T(8,128)}, u32[]{:S(2)}) copy-start(f32[512,128]{1,0:T(8,128)} %constant.61.clone.cos_c) | copy-start | bytes 786436
  24.0 39.5 %copy-start.11 = (bf16[256,128]{1,0:T(8,128)(2,1)S(1)}, bf16[256,128]{1,0:T(8,128)(2,1)}, u32[]{:S(2)}) copy-start(bf16[256,128]{1,0:T(8,128)(2,1)} %constant.71.clone.bl) | copy-start | bytes 196612
  24.0 39.5 %copy-start.12 = (bf16[256,128]{1,0:T(8,128)(2,1)S(1)}, bf16[256,128]{1,0:T(8,128)(2,1)}, u32[]{:S(2)}) copy-start(bf16[256,128]{1,0:T(8,128)(2,1)} %constant.70.clone.bh) | copy-start | bytes 196612
  24.0 39.4 %copy-start.13 = (f32[32,128]{1,0:T(8,128)S(1)}, f32[32,128]{1,0:T(8,128)}, u32[]{:S(2)}) copy-start(f32[32,128]{1,0:T(8,128)} %constant.64.clone.sin_r) | copy-start | bytes 49156
  24.0 39.4 %copy-start.14 = (f32[32,128]{1,0:T(8,128)S(1)}, f32[32,128]{1,0:T(8,128)}, u32[]{:S(2)}) copy-start(f32[32,128]{1,0:T(8,128)} %constant.63.clone.cos_r) | copy-start | bytes 49156
  24.0 39.4 %copy-start.15 = (f32[16,128]{1,0:T(8,128)S(1)}, f32[16,128]{1,0:T(8,128)}, u32[]{:S(2)}) copy-start(f32[16,128]{1,0:T(8,128)} %constant.66.clone.sin_k) | copy-start | bytes 24580
  24.1 39.4 %copy-start.16 = (f32[16,128]{1,0:T(8,128)S(1)}, f32[16,128]{1,0:T(8,128)}, u32[]{:S(2)}) copy-start(f32[16,128]{1,0:T(8,128)} %constant.65.clone.cos_k) | copy-start | bytes 24580
  25.1 38.4 %copy-start = (bf16[256,512]{1,0:T(8,128)(2,1)S(1)}, bf16[256,512]{1,0:T(8,128)(2,1)}, u32[]{:S(2)}) copy-start(bf16[256,512]{1,0:T(8,128)(2,1)} %constant.69.clone.fl) | copy-start | bytes 786436
  25.2 38.4 %copy-start.1 = (bf16[256,512]{1,0:T(8,128)(2,1)S(1)}, bf16[256,512]{1,0:T(8,128)(2,1)}, u32[]{:S(2)}) copy-start(bf16[256,512]{1,0:T(8,128)(2,1)} %constant.68.clone.fh) | copy-start | bytes 786436
  25.2 38.4 %copy-start.2 = (f32[512,128]{1,0:T(8,128)S(1)}, f32[512,128]{1,0:T(8,128)}, u32[]{:S(2)}) copy-start(f32[512,128]{1,0:T(8,128)} %constant.67.clone.decay) | copy-start | bytes 786436
  25.2 38.4 %copy-start.3 = (f32[512,128]{1,0:T(8,128)S(1)}, f32[512,128]{1,0:T(8,128)}, u32[]{:S(2)}) copy-start(f32[512,128]{1,0:T(8,128)} %constant.62.clone.sin_c) | copy-start | bytes 786436
  66.8 26.1 %copy-start.5 = (bf16[256,512]{1,0:T(8,128)(2,1)S(1)}, bf16[256,512]{1,0:T(8,128)(2,1)}, u32[]{:S(2)}) copy-start(bf16[256,512]{1,0:T(8,128)(2,1)} %constant.73.clone.low) | copy-start | bytes 786436
  66.8 26.1 %copy-start.6 = (bf16[256,512]{1,0:T(8,128)(2,1)S(1)}, bf16[256,512]{1,0:T(8,128)(2,1)}, u32[]{:S(2)}) copy-start(bf16[256,512]{1,0:T(8,128)(2,1)} %constant.72.clone.high) | copy-start | bytes 786436

commit v4 on v3

--- a/solution.py
+++ b/solution.py
@@ -150,82 +150,88 @@
                 out[pl.ds((4 * t + j) * 2 + part, R, stride=2 * C), :] = piece
 
 
-def swapped(z):
-    return pltpu.roll(z, 64, 1)
-
-
-def packed_dft(values, signs):
-    n = len(values)
-    if n == 1:
-        return values
-    even, odd = packed_dft(values[0::2], signs), packed_dft(values[1::2], signs)
-    for k in range(1, n // 2):
-        c, s = unit(k, n, 1)
-        turned = swapped(odd[k]) * (signs if s == 1.0 else signs * s)
-        odd[k] = turned if c == 0.0 else odd[k] * c + turned
-    return [e + o for e, o in zip(even, odd)] + [e - o for e, o in zip(even, odd)]
-
-
 def x_section(
-    place, lines, cos_c, sin_c, cos_r, sin_r, cos_k, sin_k, decay, fh, fl, bh, bl, out, a_re, a_im, cos_i, sin_i, wide
+    place, lines, cos_c, sin_c, cos_r, sin_r, cos_k, sin_k, decay, fh, fl, bh, bl, out, a_re, a_im, cos_i, sin_i, wide, gh, gl, late_c, late_s
 ):
-    back = (LANES - 32 * (place[1] & 3)) & (LANES - 1)
+    for part in range(2):
+        for slot in range(4):
+            here = slice(LANES * part + 32 * slot, LANES * part + 32 * (slot + 1))
+            there = pl.ds(pl.multiple_of(LANES * part + 32 * ((slot + place[1]) & 3), 32), 32)
+            gh[there, :] = fh[here, :]
+            gl[there, :] = fl[here, :]
     for h in range(2):
         values = [
-            tuple(
-                pltpu.roll(lines[pl.ds(32 * r + 16 * h + part, 8, stride=2), :], back, 1) for part in range(2)
-            )
-            for r in range(R)
+            tuple(lines[pl.ds(32 * r + 16 * h + part, 8, stride=2), :] for part in range(2)) for r in range(R)
         ]
         for k, (re, im) in enumerate(dft(values, -1)):
-            a_re[k * C + 8 * h : k * C + 8 * h + 8, :] = re
-            a_im[k * C + 8 * h : k * C + 8 * h + 8, :] = im
-    signs = jnp.where(lane_of((8, LANES)) < 64, -1.0, 1.0)
+            a_re[k * 24 + 8 * h : k * 24 + 8 * h + 8, :] = re
+            a_im[k * 24 + 8 * h : k * 24 + 8 * h + 8, :] = im
+
+    def turn_c(c, h):
+        rows = slice((c - 1) * R + 8 * h, (c - 1) * R + 8 * h + 8)
+        if c <= 8:
+            return cos_c[rows, :], sin_c[rows, :]
+        rows = slice((c - 9) * R + 8 * h, (c - 9) * R + 8 * h + 8)
+        return late_c[rows, :], late_s[rows, :]
+
     for h in range(4):
         values = []
         for c in range(C):
-            rows = slice(c * R + 8 * h, c * R + 8 * h + 8)
-            re, im = a_re[pl.ds(8 * h * C + c, 8, stride=C), :], a_im[pl.ds(8 * h * C + c, 8, stride=C), :]
+            re, im = a_re[pl.ds(8 * h * 24 + c, 8, stride=24), :], a_im[pl.ds(8 * h * 24 + c, 8, stride=24), :]
+            if c > 8:
+                (u, v), (w, z) = turn_c(c - 8, h), turn_c(8, h)
+                rows = slice((c - 9) * R + 8 * h, (c - 9) * R + 8 * h + 8)
+                late_c[rows, :], late_s[rows, :] = u * w - v * z, u * z + v * w
             if c:
-                u, v = cos_c[rows, :], sin_c[rows, :]
+                u, v = turn_c(c, h)
                 re, im = re * u + im * v, im * u - re * v
             values.append((re, im))
         for k, (re, im) in enumerate(dft(values, -1)):
-            rows = slice(k * R + 8 * h, k * R + 8 * h + 8)
+            rows = slice(h * LANES + 8 * k, h * LANES + 8 * k + 8)
             u, v = cos_r[8 * h : 8 * h + 8, :], sin_r[8 * h : 8 * h + 8, :]
             if k:
                 c, d = cos_k[k : k + 1, :], sin_k[k : k + 1, :]
                 u, v = u * c - v * d, u * d + v * c
-            cos_i[rows, :], sin_i[rows, :] = u, v * signs
+            cos_i[rows, :], sin_i[rows, :] = u, v
             wide[rows, :LANES] = re * u + im * v
             wide[rows, LANES:] = im * u - re * v
     along_y, normal = column_factors(place)
-    for t in range(4):
-        rows = slice(t * LANES, (t + 1) * LANES)
-        spectra = dot(halves(wide[rows, :]), (fh[...], fl[...]))
-        linear = decay[rows, :] + along_y
-        grown = jnp.exp(linear * (0.5 * TIME_STEP))
-        g, f = grown * (1.0 / (N * N)), (grown - 1.0) / linear * normal
-        re = g * spectra[:, :LANES] + f * spectra[:, 2 * LANES : 3 * LANES]
-        im = g * spectra[:, LANES : 2 * LANES] + f * spectra[:, 3 * LANES :]
-        advanced = halves(jnp.concatenate([re, im], axis=1))
-        wide[rows, :LANES] = dot(advanced, (bh[...], bl[...]))
-    for h in range(4):
+    low_lanes = lane_of((8, LANES)) < 64
+    for g in range(2):
+        advanced = []
+        for h in (2 * g, 2 * g + 1):
+            rows = slice(h * LANES, (h + 1) * LANES)
+            spectra = dot(halves(wide[rows, :]), (gh[...], gl[...]))
+            linear = decay[rows, :] + along_y
+            grown = jnp.exp(linear * (0.5 * TIME_STEP))
+            growth, forcing = grown * (1.0 / (N * N)), (grown - 1.0) / linear * normal
+            advanced.append(growth * spectra[:, :LANES] + forcing * spectra[:, 2 * LANES : 3 * LANES])
+            advanced.append(growth * spectra[:, LANES : 2 * LANES] + forcing * spectra[:, 3 * LANES :])
+        both = dot(halves(jnp.concatenate(advanced, axis=1)), (bh[...], bl[...]))
         values = []
         for k in range(C):
-            rows = slice(k * R + 8 * h, k * R + 8 * h + 8)
-            z = wide[rows, :LANES]
-            values.append(z * cos_i[rows, :] + swapped(z) * sin_i[rows, :])
-        for c, z in enumerate(packed_dft(values, signs)):
-            rows = slice(c * R + 8 * h, c * R + 8 * h + 8)
-            if c:
-                z = z * cos_c[rows, :] + swapped(z) * (sin_c[rows, :] * signs)
-            a_re[pl.ds(8 * h * C + c, 8, stride=C), :] = z
+            rows = [slice(h * LANES + 8 * k, h * LANES + 8 * k + 8) for h in (2 * g, 2 * g + 1)]
+            u, v = (jnp.where(low_lanes, t[rows[0], :], t[rows[1], :]) for t in (cos_i, sin_i))
+            re, im = both[8 * k : 8 * k + 8, :LANES], both[8 * k : 8 * k + 8, LANES:]
+            values.append((re * u - im * v, im * u + re * v))
+        values = dft(values, 1)
+        for c in range(1, C):
+            first, second = turn_c(c, 2 * g), turn_c(c, 2 * g + 1)
+            u, v = jnp.where(low_lanes, first[0], second[0]), jnp.where(low_lanes, first[1], second[1])
+            re, im = values[c]
+            values[c] = re * u - im * v, im * u + re * v
+        for c in range(8):
+            for part, kept in enumerate((a_re, a_im)):
+                one, two = values[c][part], values[c + 8][part]
+                kept[pl.ds(128 * g + c, 8, stride=8), :] = jnp.where(low_lanes, one, pltpu.roll(two, 64, 1))
+                kept[pl.ds(128 * g + 64 + c, 8, stride=8), :] = jnp.where(low_lanes, pltpu.roll(one, 64, 1), two)
     on = 16 * (place[1] & 7)
-    for h in range(2):
-        values = [a_re[k * C + 8 * h : k * C + 8 * h + 8, :] for k in range(R)]
-        for r, z in enumerate(packed_dft(values, signs)):
-            out[r * C + 8 * h : r * C + 8 * h + 8, :] = pltpu.roll(z, on, 1)
+    values = [(a_re[8 * k : 8 * k + 8, :], a_im[8 * k : 8 * k + 8, :]) for k in range(R)]
+    for r, (re, im) in enumerate(dft(values, 1)):
+        one = jnp.where(low_lanes, re, pltpu.roll(im, 64, 1))
+        two = jnp.where(low_lanes, pltpu.roll(re, 64, 1), im)
+        out[r * C : r * C + 8, :] = pltpu.roll(one, on, 1)
+        out[r * C + 8 : r * C + 16, :] = pltpu.roll(two, on, 1)
 
 
 def y_backward(pieces, cos_y, sin_y, high, low, out, spectrum, turned):
@@ -263,10 +269,9 @@
     c, s = np.cos(turn_m), np.sin(turn_m)
     y_matrix = np.block([[c, -s], [s, c]])
     y_inverse = 2 * np.block([[c.T, s.T], [-s.T, c.T]])
-    k_r = np.tile(np.arange(R), C)
-    outer = np.repeat(np.arange(C), R)
     ones = np.ones((1, LANES))
-    angle = 2 * np.pi / D * (outer * k_r % D)[:, None] * ones
+    outer = np.arange(1, 9)[:, None] * np.arange(R)[None, :]
+    angle = 2 * np.pi / D * outer.reshape(-1, 1) * ones
     cos_c, sin_c = np.cos(angle), np.sin(angle)
     lane_i = (np.arange(LANES) % I)[None, :]
     angle = 2 * np.pi / N * (np.arange(R)[:, None] * lane_i)
@@ -276,28 +281,26 @@
     angle = 2 * np.pi / I * (np.arange(I)[:, None] * np.arange(I)[None, :] % I)
     c, s = np.cos(angle), np.sin(angle)
     forward = np.zeros((2, LANES, 2, 2, LANES))
-    backward = np.zeros((2, LANES, LANES))
+    backward = np.zeros((2, 2, LANES, 2, LANES))
     for slot in range(5):
         for field in range(2):
             here = slice(16 * slot + I * field, 16 * slot + I * field + I)
-            if slot < 4:
-                there = slice(64 + here.start, 64 + here.stop)
-                backward[0, here, here], backward[1, here, here] = c, -s
-                backward[0, here, there], backward[1, here, there] = s, c
-            else:
-                start = slice(I * field, I * field + I)
-                there = slice(64 + I * field, 64 + I * field + I)
-                backward[0, here, start], backward[1, here, start] = -s, -c
-                backward[0, here, there], backward[1, here, there] = c, -s
+            for g in range(2):
+                there = slice(64 * g + 16 * (slot % 4) + I * field, 64 * g + 16 * (slot % 4) + I * field + I)
+                turn_i = ((c, -s), (s, c)) if slot < 4 else ((-s, -c), (c, -s))
+                for part in range(2):
+                    backward[g, 0, here, part, there] += turn_i[part][0]
+                    backward[g, 1, here, part, there] += turn_i[part][1]
             for kind, taken in enumerate((field, 2)):
                 start = 32 * slot + I * taken if slot < 4 else 32 * taken + 3 * I
                 there = slice(start, start + I)
                 forward[0, there, kind, 0, here], forward[1, there, kind, 0, here] = c, s
                 forward[0, there, kind, 1, here], forward[1, there, kind, 1, here] = -s, c
     forward = forward.reshape(2 * LANES, 4 * LANES)
-    backward = backward.reshape(2 * LANES, LANES)
+    backward = backward.reshape(4 * LANES, 2 * LANES)
     lane = np.arange(LANES)[None, :]
-    p = np.arange(D)[:, None] + D * (lane % I)
+    row = np.arange(D)[:, None]
+    p = 8 * (row // LANES) + row % 8 + R * (row % LANES // 8) + D * (lane % I)
     angular = 2 * np.pi * np.where(2 * p < N, p, p - N)
     decay = -np.where(lane // I % 2 == 0, SUBSTRATE_DIFFUSION, ACTIVATOR_DIFFUSION) * angular**2
 
@@ -334,7 +337,7 @@
         out_shape=jax.ShapeDtypeStruct(out_shape, jnp.float32),
         in_specs=spaces,
         out_specs=pl.BlockSpec(memory_space=pltpu.VMEM),
-        scratch_shapes=[pltpu.VMEM(shape, jnp.float32) for shape in scratch],
+        scratch_shapes=[pltpu.VMEM(shape[:2], *shape[2:] or (jnp.float32,)) for shape in scratch],
         compiler_params=pltpu.CompilerParams(vmem_limit_bytes=48 * 1024 * 1024),
     )(*operands)
 
@@ -347,7 +350,8 @@
     fields = lax.all_to_all(fields, "col", 0, 0, tiled=True)
     pieces = call(y_forward, (2 * D, LANES), [(D, 2 * M)], fields, *along_y)
     lines = lax.all_to_all(pieces.reshape(D, 2, LANES), ALL, 0, 0, tiled=True).reshape(2 * D, LANES)
-    scratch = [(D, LANES)] * 4 + [(D, 2 * LANES)]
+    scratch = [(24 * R, LANES)] * 2 + [(D, LANES)] * 2 + [(D, 2 * LANES)]
+    scratch += [(2 * LANES, 4 * LANES, jnp.bfloat16)] * 2 + [(7 * R, LANES)] * 2
     pieces = call(x_section, (D, LANES), scratch, place, lines, *along_x, scalars=1)
     pieces = lax.all_to_all(pieces.reshape(D, 1, LANES), ALL, 0, 0, tiled=True).reshape(D, LANES)
     fields = call(y_backward, (C, 2 * I, M), [(M, M), (M, 2 * M)], pieces, *back_y)

time: 110 us -> 109 us (level)
  no operation moved by 1% of the time
where the time goes in v4:
time: 109 us; the launch traced here: 108 us
  blocking collectives  101 us (93%)
  Pallas kernels  3.99 us (4%)
    all_to_all x1, blocking collectives, on_device(): lax.all_to_all(pieces.reshape(D, 2, LANES), ALL, 0, 0, tiled=True)  38.3 us
    all_to_all x2, blocking collectives, on_device(): fields = lax.all_to_all(fields, 'col', 0, 0, tiled=True)  37.1 us
    all_to_all x1, blocking collectives, on_device(): lax.all_to_all(pieces.reshape(D, 1, LANES), ALL, 0, 0, tiled=True)  26.1 us
    pallas_call x3, Pallas kernels, call(): pl.pallas_call(body, out_shape=jax.ShapeDtypeStruct(out_shape, jnp.float3...  3.99 us

profile of v4, /device:TPU:1, one launch (start us, length us, event | category | flops | bytes accessed | tf_op | source)
XLA Modules:
  0.0 108.2 jit_solution(17026453843382943992)
XLA Ops:
  0.6 0.1 pad_add_fusion.place
  0.7 1.0 pad_maximum_fusion
  1.7 0.0 copy-start.2
  1.7 0.0 copy-start.3
  1.7 22.2 %all_to_all.20.fields = f32[16,16,256]{2,1,0:T(8,128)S(1)} all-to-all(f32[16,16,256]{2,1,0:T(8,128)S(1)} %pad_maximum_fusion), channel_id=1, replica_groups=mesh['row_0'=8,'row_1'=2,'row_2'=2,'col'=16] {'col'}, dimensions={0} | all-to-all | bytes 524288 | tf_op jit(solution)/shard_map/all_to_all | solution.py:350
  24.0 0.0 copy-start.8
  24.0 0.0 copy-start.9
  24.0 0.0 copy-start.10
  24.0 0.0 copy-start.13
  24.0 0.0 copy-start.14
  24.0 0.0 copy-start.15
  24.1 0.0 copy-start.16
  24.1 1.1 shard_map.194
  25.1 0.0 copy-start.4
  25.2 0.0 copy-start.5
  25.2 0.0 copy-start.6
  25.2 0.0 copy-start.7
  25.2 38.3 %all_to_all.21 = f32[512,2,128]{2,1,0:T(2,128)S(1)} all-to-all(f32[512,2,128]{2,1,0:T(2,128)S(1)} %bitcast.15), channel_id=1, replica_groups=mesh['row_0'=8,'row_1'=2,'row_2'=2,'col'=16] {'row_0','row_1','row_2','c..., dimensions={0} | all-to-all | bytes 1048576 | tf_op jit(solution)/shard_map/all_to_all | solution.py:352
  63.5 2.3 %shard_map.195 = f32[512,128]{1,0:T(8,128)S(1)} custom-call(s32[2]{0:T(128)S(1)} %pad_add_fusion.place, f32[1024,128]{1,0:T(8,128)S(1)} %bitcast.14, f32[256,128]{1,0:T(8,128)S(1)} %copy-done.10, f32[256,128]{1,0:T(8,128)S(1)} %copy-done.9, f32[32,128]{1,0:T(8,128)S(1)} %copy-done.14, f32[32,128]{1,0:T(8,128)S(1)} %copy-done.13, f32[16,128]{1,0:T(8,128)S(1)} %copy-done.16, ...), custom_call_target="tpu_custom_call" | custom-call | tf_op jit(solution)/shard_map/pallas_call | solution.py:335
  65.9 0.0 copy-start.1
  65.9 26.1 %all_to_all.22 = f32[512,1,128]{2,1,0:T(1,128)S(1)} all-to-all(f32[512,1,128]{2,1,0:T(1,128)S(1)} %bitcast.17), channel_id=1, replica_groups=mesh['row_0'=8,'row_1'=2,'row_2'=2,'col'=16] {'row_0','row_1','row_2','c..., dimensions={0} | all-to-all | bytes 524288 | tf_op jit(solution)/shard_map/all_to_all | solution.py:356
  91.9 0.6 shard_map.196
  92.6 14.9 %all_to_all.23 = f32[16,16,256]{2,1,0:T(8,128)S(1)} all-to-all(f32[16,16,256]{2,1,0:T(8,128)S(1)} %shard_map.196), channel_id=1, replica_groups=mesh['row_0'=8,'row_1'=2,'row_2'=2,'col'=16] {'col'}, dimensions={0} | all-to-all | bytes 524288 | tf_op jit(solution)/shard_map/all_to_all | solution.py:358
  107.4 0.7 slice_bitcast_fusion
  (20 shorter events, 0.0 us)
Async XLA Ops:
  0.7 23.2 %copy-start.11 = (f32[16,256]{1,0:T(8,128)S(1)}, f32[16,256]{1,0:T(8,128)}, u32[]{:S(2)}) copy-start(f32[16,256]{1,0:T(8,128)} %constant.58.clone.sin_y) | copy-start | bytes 49156
  0.7 23.3 %copy-start.12 = (f32[16,256]{1,0:T(8,128)S(1)}, f32[16,256]{1,0:T(8,128)}, u32[]{:S(2)}) copy-start(f32[16,256]{1,0:T(8,128)} %constant.57.clone.cos_y) | copy-start | bytes 49156
  1.7 22.2 %copy-start.2 = (bf16[512,256]{1,0:T(8,128)(2,1)S(1)}, bf16[512,256]{1,0:T(8,128)(2,1)}, u32[]{:S(2)}) copy-start(bf16[512,256]{1,0:T(8,128)(2,1)} %constant.60.clone.low) | copy-start | bytes 786436
  1.7 22.2 %copy-start.3 = (bf16[512,256]{1,0:T(8,128)(2,1)S(1)}, bf16[512,256]{1,0:T(8,128)(2,1)}, u32[]{:S(2)}) copy-start(bf16[512,256]{1,0:T(8,128)(2,1)} %constant.59.clone.high) | copy-start | bytes 786436
  24.0 39.5 %copy-start.8 = (f32[512,128]{1,0:T(8,128)S(1)}, f32[512,128]{1,0:T(8,128)}, u32[]{:S(2)}) copy-start(f32[512,128]{1,0:T(8,128)} %constant.67.clone.decay) | copy-start | bytes 786436
  24.0 39.5 %copy-start.9 = (f32[256,128]{1,0:T(8,128)S(1)}, f32[256,128]{1,0:T(8,128)}, u32[]{:S(2)}) copy-start(f32[256,128]{1,0:T(8,128)} %constant.62.clone.sin_c) | copy-start | bytes 393220
  24.0 39.5 %copy-start.10 = (f32[256,128]{1,0:T(8,128)S(1)}, f32[256,128]{1,0:T(8,128)}, u32[]{:S(2)}) copy-start(f32[256,128]{1,0:T(8,128)} %constant.61.clone.cos_c) | copy-start | bytes 393220
  24.0 39.4 %copy-start.13 = (f32[32,128]{1,0:T(8,128)S(1)}, f32[32,128]{1,0:T(8,128)}, u32[]{:S(2)}) copy-start(f32[32,128]{1,0:T(8,128)} %constant.64.clone.sin_r) | copy-start | bytes 49156
  24.0 39.4 %copy-start.14 = (f32[32,128]{1,0:T(8,128)S(1)}, f32[32,128]{1,0:T(8,128)}, u32[]{:S(2)}) copy-start(f32[32,128]{1,0:T(8,128)} %constant.63.clone.cos_r) | copy-start | bytes 49156
  24.0 39.4 %copy-start.15 = (f32[16,128]{1,0:T(8,128)S(1)}, f32[16,128]{1,0:T(8,128)}, u32[]{:S(2)}) copy-start(f32[16,128]{1,0:T(8,128)} %constant.66.clone.sin_k) | copy-start | bytes 24580
  24.1 39.4 %copy-start.16 = (f32[16,128]{1,0:T(8,128)S(1)}, f32[16,128]{1,0:T(8,128)}, u32[]{:S(2)}) copy-start(f32[16,128]{1,0:T(8,128)} %constant.65.clone.cos_k) | copy-start | bytes 24580
  25.1 38.4 %copy-start.4 = (bf16[512,256]{1,0:T(8,128)(2,1)S(1)}, bf16[512,256]{1,0:T(8,128)(2,1)}, u32[]{:S(2)}) copy-start(bf16[512,256]{1,0:T(8,128)(2,1)} %constant.71.clone.bl) | copy-start | bytes 786436
  25.2 38.4 %copy-start.5 = (bf16[512,256]{1,0:T(8,128)(2,1)S(1)}, bf16[512,256]{1,0:T(8,128)(2,1)}, u32[]{:S(2)}) copy-start(bf16[512,256]{1,0:T(8,128)(2,1)} %constant.70.clone.bh) | copy-start | bytes 786436
  25.2 38.4 %copy-start.6 = (bf16[256,512]{1,0:T(8,128)(2,1)S(1)}, bf16[256,512]{1,0:T(8,128)(2,1)}, u32[]{:S(2)}) copy-start(bf16[256,512]{1,0:T(8,128)(2,1)} %constant.69.clone.fl) | copy-start | bytes 786436
  25.2 38.4 %copy-start.7 = (bf16[256,512]{1,0:T(8,128)(2,1)S(1)}, bf16[256,512]{1,0:T(8,128)(2,1)}, u32[]{:S(2)}) copy-start(bf16[256,512]{1,0:T(8,128)(2,1)} %constant.68.clone.fh) | copy-start | bytes 786436
  65.8 26.1 %copy-start = (bf16[256,512]{1,0:T(8,128)(2,1)S(1)}, bf16[256,512]{1,0:T(8,128)(2,1)}, u32[]{:S(2)}) copy-start(bf16[256,512]{1,0:T(8,128)(2,1)} %constant.73.clone.low) | copy-start | bytes 786436
  65.9 26.1 %copy-start.1 = (bf16[256,512]{1,0:T(8,128)(2,1)S(1)}, bf16[256,512]{1,0:T(8,128)(2,1)}, u32[]{:S(2)}) copy-start(bf16[256,512]{1,0:T(8,128)(2,1)} %constant.72.clone.high) | copy-start | bytes 786436

commit v5 on v4

--- a/solution.py
+++ b/solution.py
@@ -10,7 +10,8 @@
 from jax.sharding import PartitionSpec as P
 
 ROW = ("row_0", "row_1", "row_2")
-ALL = ("row_0", "row_1", "row_2", "col")
+ROW_BY_CORE = ("row_2", "row_0", "row_1")
+ALL = (*ROW_BY_CORE, "col")
 
 FEED_RATE = 0.037
 KILL_RATE = 0.06
@@ -150,6 +151,10 @@
                 out[pl.ds((4 * t + j) * 2 + part, R, stride=2 * C), :] = piece
 
 
+def sent(r):
+    return r % 2 * (R // 2) + r // 2
+
+
 def x_section(
     place, lines, cos_c, sin_c, cos_r, sin_r, cos_k, sin_k, decay, fh, fl, bh, bl, out, a_re, a_im, cos_i, sin_i, wide, gh, gl, late_c, late_s
 ):
@@ -161,7 +166,8 @@
             gl[there, :] = fl[here, :]
     for h in range(2):
         values = [
-            tuple(lines[pl.ds(32 * r + 16 * h + part, 8, stride=2), :] for part in range(2)) for r in range(R)
+            tuple(lines[pl.ds(32 * sent(r) + 16 * h + part, 8, stride=2), :] for part in range(2))
+            for r in range(R)
         ]
         for k, (re, im) in enumerate(dft(values, -1)):
             a_re[k * 24 + 8 * h : k * 24 + 8 * h + 8, :] = re
@@ -230,8 +236,9 @@
     for r, (re, im) in enumerate(dft(values, 1)):
         one = jnp.where(low_lanes, re, pltpu.roll(im, 64, 1))
         two = jnp.where(low_lanes, pltpu.roll(re, 64, 1), im)
-        out[r * C : r * C + 8, :] = pltpu.roll(one, on, 1)
-        out[r * C + 8 : r * C + 16, :] = pltpu.roll(two, on, 1)
+        row = C * sent(r)
+        out[row : row + 8, :] = pltpu.roll(one, on, 1)
+        out[row + 8 : row + 16, :] = pltpu.roll(two, on, 1)
 
 
 def y_backward(pieces, cos_y, sin_y, high, low, out, spectrum, turned):
@@ -344,7 +351,7 @@
 
 def on_device(substrate, activator):
     along_y, along_x, back_y = tables()
-    place = jnp.stack([lax.axis_index(ROW), lax.axis_index("col")])
+    place = jnp.stack([lax.axis_index(ROW_BY_CORE), lax.axis_index("col")])
     fields = jnp.concatenate([substrate.reshape(C, I, M), activator.reshape(C, I, M)], axis=1)
     fields, place = lax.optimization_barrier((fields, place))
     fields = lax.all_to_all(fields, "col", 0, 0, tiled=True)

time: 109 us -> 109 us (level)
  no operation moved by 1% of the time
where the time goes in v5:
time: 109 us; the launch traced here: 108 us
  blocking collectives  102 us (94%)
  Pallas kernels  3.99 us (4%)
    all_to_all x1, blocking collectives, on_device(): lax.all_to_all(pieces.reshape(D, 2, LANES), ALL, 0, 0, tiled=True)  38.5 us
    all_to_all x2, blocking collectives, on_device(): fields = lax.all_to_all(fields, 'col', 0, 0, tiled=True)  37.4 us
    all_to_all x1, blocking collectives, on_device(): lax.all_to_all(pieces.reshape(D, 1, LANES), ALL, 0, 0, tiled=True)  25.9 us
    pallas_call x3, Pallas kernels, call(): pl.pallas_call(body, out_shape=jax.ShapeDtypeStruct(out_shape, jnp.float3...  3.99 us

profile of v5, /device:TPU:1, one launch (start us, length us, event | category | flops | bytes accessed | tf_op | source)
XLA Modules:
  0.0 108.5 jit_solution(8537477774141946132)
XLA Ops:
  0.6 0.1 pad_add_fusion.place
  0.7 1.0 pad_maximum_fusion
  1.7 0.0 copy-start.2
  1.7 0.0 copy-start.3
  1.7 22.2 %all_to_all.20.fields = f32[16,16,256]{2,1,0:T(8,128)S(1)} all-to-all(f32[16,16,256]{2,1,0:T(8,128)S(1)} %pad_maximum_fusion), channel_id=1, replica_groups=mesh['row_0'=8,'row_1'=2,'row_2'=2,'col'=16] {'col'}, dimensions={0} | all-to-all | bytes 524288 | tf_op jit(solution)/shard_map/all_to_all | solution.py:357
  24.0 0.0 copy-start.8
  24.0 0.0 copy-start.9
  24.0 0.0 copy-start.10
  24.0 0.0 copy-start.13
  24.0 0.0 copy-start.14
  24.0 0.0 copy-start.15
  24.1 0.0 copy-start.16
  24.1 1.1 shard_map.194
  25.1 0.0 copy-start.4
  25.2 0.0 copy-start.5
  25.2 0.0 copy-start.6
  25.2 0.0 copy-start.7
  25.2 38.5 %all_to_all.21 = f32[512,2,128]{2,1,0:T(2,128)S(1)} all-to-all(f32[512,2,128]{2,1,0:T(2,128)S(1)} %bitcast.15), channel_id=1, replica_groups=mesh['row_0'=8,'row_1'=2,'row_2'=2,'col'=16] {'row_2','row_0','row_1','c..., dimensions={0} | all-to-all | bytes 1048576 | tf_op jit(solution)/shard_map/all_to_all | solution.py:359
  63.8 2.3 %shard_map.195 = f32[512,128]{1,0:T(8,128)S(1)} custom-call(s32[2]{0:T(128)S(1)} %pad_add_fusion.place, f32[1024,128]{1,0:T(8,128)S(1)} %bitcast.14, f32[256,128]{1,0:T(8,128)S(1)} %copy-done.10, f32[256,128]{1,0:T(8,128)S(1)} %copy-done.9, f32[32,128]{1,0:T(8,128)S(1)} %copy-done.14, f32[32,128]{1,0:T(8,128)S(1)} %copy-done.13, f32[16,128]{1,0:T(8,128)S(1)} %copy-done.16, ...), custom_call_target="tpu_custom_call" | custom-call | tf_op jit(solution)/shard_map/pallas_call | solution.py:342
  66.1 0.0 copy-start.1
  66.1 25.9 %all_to_all.22 = f32[512,1,128]{2,1,0:T(1,128)S(1)} all-to-all(f32[512,1,128]{2,1,0:T(1,128)S(1)} %bitcast.17), channel_id=1, replica_groups=mesh['row_0'=8,'row_1'=2,'row_2'=2,'col'=16] {'row_2','row_0','row_1','c..., dimensions={0} | all-to-all | bytes 524288 | tf_op jit(solution)/shard_map/all_to_all | solution.py:363
  92.0 0.6 shard_map.196
  92.6 15.2 %all_to_all.23 = f32[16,16,256]{2,1,0:T(8,128)S(1)} all-to-all(f32[16,16,256]{2,1,0:T(8,128)S(1)} %shard_map.196), channel_id=1, replica_groups=mesh['row_0'=8,'row_1'=2,'row_2'=2,'col'=16] {'col'}, dimensions={0} | all-to-all | bytes 524288 | tf_op jit(solution)/shard_map/all_to_all | solution.py:365
  107.8 0.7 slice_bitcast_fusion
  (20 shorter events, 0.0 us)
Async XLA Ops:
  0.7 23.2 %copy-start.11 = (f32[16,256]{1,0:T(8,128)S(1)}, f32[16,256]{1,0:T(8,128)}, u32[]{:S(2)}) copy-start(f32[16,256]{1,0:T(8,128)} %constant.58.clone.sin_y) | copy-start | bytes 49156
  0.7 23.3 %copy-start.12 = (f32[16,256]{1,0:T(8,128)S(1)}, f32[16,256]{1,0:T(8,128)}, u32[]{:S(2)}) copy-start(f32[16,256]{1,0:T(8,128)} %constant.57.clone.cos_y) | copy-start | bytes 49156
  1.7 22.2 %copy-start.2 = (bf16[512,256]{1,0:T(8,128)(2,1)S(1)}, bf16[512,256]{1,0:T(8,128)(2,1)}, u32[]{:S(2)}) copy-start(bf16[512,256]{1,0:T(8,128)(2,1)} %constant.60.clone.low) | copy-start | bytes 786436
  1.7 22.2 %copy-start.3 = (bf16[512,256]{1,0:T(8,128)(2,1)S(1)}, bf16[512,256]{1,0:T(8,128)(2,1)}, u32[]{:S(2)}) copy-start(bf16[512,256]{1,0:T(8,128)(2,1)} %constant.59.clone.high) | copy-start | bytes 786436
  24.0 39.7 %copy-start.8 = (f32[512,128]{1,0:T(8,128)S(1)}, f32[512,128]{1,0:T(8,128)}, u32[]{:S(2)}) copy-start(f32[512,128]{1,0:T(8,128)} %constant.67.clone.decay) | copy-start | bytes 786436
  24.0 39.7 %copy-start.9 = (f32[256,128]{1,0:T(8,128)S(1)}, f32[256,128]{1,0:T(8,128)}, u32[]{:S(2)}) copy-start(f32[256,128]{1,0:T(8,128)} %constant.62.clone.sin_c) | copy-start | bytes 393220
  24.0 39.7 %copy-start.10 = (f32[256,128]{1,0:T(8,128)S(1)}, f32[256,128]{1,0:T(8,128)}, u32[]{:S(2)}) copy-start(f32[256,128]{1,0:T(8,128)} %constant.61.clone.cos_c) | copy-start | bytes 393220
  24.0 39.7 %copy-start.13 = (f32[32,128]{1,0:T(8,128)S(1)}, f32[32,128]{1,0:T(8,128)}, u32[]{:S(2)}) copy-start(f32[32,128]{1,0:T(8,128)} %constant.64.clone.sin_r) | copy-start | bytes 49156
  24.0 39.7 %copy-start.14 = (f32[32,128]{1,0:T(8,128)S(1)}, f32[32,128]{1,0:T(8,128)}, u32[]{:S(2)}) copy-start(f32[32,128]{1,0:T(8,128)} %constant.63.clone.cos_r) | copy-start | bytes 49156
  24.0 39.7 %copy-start.15 = (f32[16,128]{1,0:T(8,128)S(1)}, f32[16,128]{1,0:T(8,128)}, u32[]{:S(2)}) copy-start(f32[16,128]{1,0:T(8,128)} %constant.66.clone.sin_k) | copy-start | bytes 24580
  24.1 39.7 %copy-start.16 = (f32[16,128]{1,0:T(8,128)S(1)}, f32[16,128]{1,0:T(8,128)}, u32[]{:S(2)}) copy-start(f32[16,128]{1,0:T(8,128)} %constant.65.clone.cos_k) | copy-start | bytes 24580
  25.1 38.6 %copy-start.4 = (bf16[512,256]{1,0:T(8,128)(2,1)S(1)}, bf16[512,256]{1,0:T(8,128)(2,1)}, u32[]{:S(2)}) copy-start(bf16[512,256]{1,0:T(8,128)(2,1)} %constant.71.clone.bl) | copy-start | bytes 786436
  25.2 38.6 %copy-start.5 = (bf16[512,256]{1,0:T(8,128)(2,1)S(1)}, bf16[512,256]{1,0:T(8,128)(2,1)}, u32[]{:S(2)}) copy-start(bf16[512,256]{1,0:T(8,128)(2,1)} %constant.70.clone.bh) | copy-start | bytes 786436
  25.2 38.6 %copy-start.6 = (bf16[256,512]{1,0:T(8,128)(2,1)S(1)}, bf16[256,512]{1,0:T(8,128)(2,1)}, u32[]{:S(2)}) copy-start(bf16[256,512]{1,0:T(8,128)(2,1)} %constant.69.clone.fl) | copy-start | bytes 786436
  25.2 38.6 %copy-start.7 = (bf16[256,512]{1,0:T(8,128)(2,1)S(1)}, bf16[256,512]{1,0:T(8,128)(2,1)}, u32[]{:S(2)}) copy-start(bf16[256,512]{1,0:T(8,128)(2,1)} %constant.68.clone.fh) | copy-start | bytes 786436
  66.1 25.9 %copy-start = (bf16[256,512]{1,0:T(8,128)(2,1)S(1)}, bf16[256,512]{1,0:T(8,128)(2,1)}, u32[]{:S(2)}) copy-start(bf16[256,512]{1,0:T(8,128)(2,1)} %constant.73.clone.low) | copy-start | bytes 786436
  66.1 25.9 %copy-start.1 = (bf16[256,512]{1,0:T(8,128)(2,1)S(1)}, bf16[256,512]{1,0:T(8,128)(2,1)}, u32[]{:S(2)}) copy-start(bf16[256,512]{1,0:T(8,128)(2,1)} %constant.72.clone.high) | copy-start | bytes 786436

commit v6 on v4

--- a/solution.py
+++ b/solution.py
@@ -151,8 +151,9 @@
 
 
 def x_section(
-    place, lines, cos_c, sin_c, cos_r, sin_r, cos_k, sin_k, decay, fh, fl, bh, bl, out, a_re, a_im, cos_i, sin_i, wide, gh, gl, late_c, late_s
+    lines, cos_c, sin_c, cos_r, sin_r, cos_k, sin_k, decay, fh, fl, bh, bl, out, a_re, a_im, cos_i, sin_i, wide, gh, gl, late_c, late_s
 ):
+    place = lax.axis_index(ROW), lax.axis_index("col")
     for part in range(2):
         for slot in range(4):
             here = slice(LANES * part + 32 * slot, LANES * part + 32 * (slot + 1))
@@ -330,33 +331,72 @@
     return -diffusion * (angular * angular) - decay, jnp.where(substrate, -normalize, normalize)
 
 
-def call(body, out_shape, scratch, *operands, scalars=0):
-    spaces = [pl.BlockSpec(memory_space=pltpu.SMEM if k < scalars else pltpu.VMEM) for k in range(len(operands))]
+def call(body, out_shape, scratch, *operands):
     return pl.pallas_call(
         body,
         out_shape=jax.ShapeDtypeStruct(out_shape, jnp.float32),
-        in_specs=spaces,
+        in_specs=[pl.BlockSpec(memory_space=pltpu.VMEM) for _ in operands],
         out_specs=pl.BlockSpec(memory_space=pltpu.VMEM),
         scratch_shapes=[pltpu.VMEM(shape[:2], *shape[2:] or (jnp.float32,)) for shape in scratch],
         compiler_params=pltpu.CompilerParams(vmem_limit_bytes=48 * 1024 * 1024),
     )(*operands)
 
 
+def stack_fields(substrate, activator, out, first, second):
+    copies = (
+        pltpu.make_async_copy(substrate, out.at[:, :I, :], first),
+        pltpu.make_async_copy(activator, out.at[:, I:, :], second),
+    )
+    for copy in copies:
+        copy.start()
+    for copy in copies:
+        copy.wait()
+
+
+def split_fields(fields, substrate, activator, first, second):
+    copies = (
+        pltpu.make_async_copy(fields.at[:, :I, :], substrate, first),
+        pltpu.make_async_copy(fields.at[:, I:, :], activator, second),
+    )
+    for copy in copies:
+        copy.start()
+    for copy in copies:
+        copy.wait()
+
+
 def on_device(substrate, activator):
     along_y, along_x, back_y = tables()
-    place = jnp.stack([lax.axis_index(ROW), lax.axis_index("col")])
-    fields = jnp.concatenate([substrate.reshape(C, I, M), activator.reshape(C, I, M)], axis=1)
-    fields, place = lax.optimization_barrier((fields, place))
+    whole = pl.BlockSpec(memory_space=pltpu.VMEM)
+    outside = pl.BlockSpec(memory_space=pl.ANY)
+    one = jax.ShapeDtypeStruct((C, I, M), jnp.float32)
+    small = pltpu.CompilerParams(vmem_limit_bytes=4 * 1024 * 1024)
+    flags = [pltpu.SemaphoreType.DMA, pltpu.SemaphoreType.DMA]
+    fields = pl.pallas_call(
+        stack_fields,
+        out_shape=jax.ShapeDtypeStruct((C, 2 * I, M), jnp.float32),
+        in_specs=[outside, outside],
+        out_specs=whole,
+        scratch_shapes=flags,
+        compiler_params=small,
+    )(substrate.reshape(C, I, M), activator.reshape(C, I, M))
     fields = lax.all_to_all(fields, "col", 0, 0, tiled=True)
     pieces = call(y_forward, (2 * D, LANES), [(D, 2 * M)], fields, *along_y)
     lines = lax.all_to_all(pieces.reshape(D, 2, LANES), ALL, 0, 0, tiled=True).reshape(2 * D, LANES)
     scratch = [(24 * R, LANES)] * 2 + [(D, LANES)] * 2 + [(D, 2 * LANES)]
     scratch += [(2 * LANES, 4 * LANES, jnp.bfloat16)] * 2 + [(7 * R, LANES)] * 2
-    pieces = call(x_section, (D, LANES), scratch, place, lines, *along_x, scalars=1)
+    pieces = call(x_section, (D, LANES), scratch, lines, *along_x)
     pieces = lax.all_to_all(pieces.reshape(D, 1, LANES), ALL, 0, 0, tiled=True).reshape(D, LANES)
     fields = call(y_backward, (C, 2 * I, M), [(M, M), (M, 2 * M)], pieces, *back_y)
     fields = lax.all_to_all(fields, "col", 0, 0, tiled=True)
-    return (fields[:, :I].reshape(C * I, M), fields[:, I:].reshape(C * I, M))
+    substrate, activator = pl.pallas_call(
+        split_fields,
+        out_shape=(one, one),
+        in_specs=[whole],
+        out_specs=(outside, outside),
+        scratch_shapes=flags,
+        compiler_params=small,
+    )(fields)
+    return substrate.reshape(C * I, M), activator.reshape(C * I, M)
 
 
 def solution(mesh):

time: 109 us -> 109 us (level)
    unnamed x34 -> x38, local copies, waits for them, and re-layouts: 0.11 us -> 1.91 us
where the time goes in v6:
time: 109 us; the launch traced here: 108 us
  blocking collectives  101 us (93%)
  Pallas kernels  4.14 us (4%)
  local copies, waits for them, and re-layouts  1.91 us (2%)
    all_to_all x1, blocking collectives, on_device(): lax.all_to_all(pieces.reshape(D, 2, LANES), ALL, 0, 0, tiled=True)  38.3 us
    all_to_all x2, blocking collectives, on_device(): fields = lax.all_to_all(fields, 'col', 0, 0, tiled=True)  37.1 us
    all_to_all x1, blocking collectives, on_device(): lax.all_to_all(pieces.reshape(D, 1, LANES), ALL, 0, 0, tiled=True)  26.1 us
    pallas_call x3, Pallas kernels, call(): pl.pallas_call(body, out_shape=jax.ShapeDtypeStruct(out_shape, jnp.float3...  3.38 us

profile of v6, /device:TPU:1, one launch (start us, length us, event | category | flops | bytes accessed | tf_op | source)
XLA Modules:
  0.0 108.3 jit_solution(6342998246213555075)
XLA Ops:
  0.6 0.9 copy-done.11
  1.5 0.9 copy-done.12
  2.4 0.1 shard_map.194
  2.5 0.0 copy-start.7
  2.5 0.0 copy-start.8
  2.5 22.2 %all_to_all.20.fields = f32[16,16,256]{2,1,0:T(8,128)S(1)} all-to-all(f32[16,16,256]{2,1,0:T(8,128)S(1)} %shard_map.194), channel_id=1, replica_groups=mesh['row_0'=8,'row_1'=2,'row_2'=2,'col'=16] {'col'}, dimensions={0} | all-to-all | bytes 524288 | tf_op jit(solution)/shard_map/all_to_all | solution.py:382
  24.8 0.0 copy-start.4
  24.8 0.0 copy-start.9
  24.8 0.0 copy-start.10
  24.8 0.0 copy-start.15
  24.8 0.0 copy-start.16
  24.8 0.0 copy-start.17
  24.8 1.1 shard_map.195
  25.9 0.0 copy-start
  25.9 0.0 copy-start.1
  25.9 0.0 copy-start.2
  26.0 0.0 copy-start.3
  26.0 38.3 %all_to_all.21 = f32[512,2,128]{2,1,0:T(2,128)S(1)} all-to-all(f32[512,2,128]{2,1,0:T(2,128)S(1)} %bitcast.11), channel_id=1, replica_groups=mesh['row_0'=8,'row_1'=2,'row_2'=2,'col'=16] {'row_0','row_1','row_2','c..., dimensions={0} | all-to-all | bytes 1048576 | tf_op jit(solution)/shard_map/all_to_all | solution.py:384
  64.3 1.7 %shard_map.196 = f32[512,128]{1,0:T(8,128)S(1)} custom-call(f32[1024,128]{1,0:T(8,128)S(1)} %bitcast.10, f32[256,128]{1,0:T(8,128)S(1)} %copy-done.10, f32[256,128]{1,0:T(8,128)S(1)} %copy-done.9, f32[32,128]{1,0:T(8,128)S(1)} %copy-done.16, f32[32,128]{1,0:T(8,128)S(1)} %copy-done.15, f32[16,128]{1,0:T(8,128)S(1)} %copy-done.18, f32[16,128]{1,0:T(8,128)S(1)} %copy-done.17, ...), custom_call_target="tpu_custom_call" | custom-call | tf_op jit(solution)/shard_map/pallas_call | solution.py:335
  66.0 0.0 copy-start.6
  66.0 26.1 %all_to_all.22 = f32[512,1,128]{2,1,0:T(1,128)S(1)} all-to-all(f32[512,1,128]{2,1,0:T(1,128)S(1)} %bitcast.12), channel_id=1, replica_groups=mesh['row_0'=8,'row_1'=2,'row_2'=2,'col'=16] {'row_0','row_1','row_2','c..., dimensions={0} | all-to-all | bytes 524288 | tf_op jit(solution)/shard_map/all_to_all | solution.py:388
  92.1 0.6 shard_map.197
  92.7 14.9 %all_to_all.23.fields = f32[16,16,256]{2,1,0:T(8,128)S(1)} all-to-all(f32[16,16,256]{2,1,0:T(8,128)S(1)} %shard_map.197), channel_id=1, replica_groups=mesh['row_0'=8,'row_1'=2,'row_2'=2,'col'=16] {'col'}, dimensions={0} | all-to-all | bytes 524288 | tf_op jit(solution)/shard_map/all_to_all | solution.py:390
  107.6 0.7 shard_map.198
  (23 shorter events, 0.1 us)
Async XLA Ops:
  0.6 0.9 copy-start.11
  1.5 0.9 copy-start.12
  2.4 22.3 %copy-start.13 = (f32[16,256]{1,0:T(8,128)S(1)}, f32[16,256]{1,0:T(8,128)}, u32[]{:S(2)}) copy-start(f32[16,256]{1,0:T(8,128)} %constant.35.clone.sin_y) | copy-start | bytes 49156
  2.4 22.3 %copy-start.14 = (f32[16,256]{1,0:T(8,128)S(1)}, f32[16,256]{1,0:T(8,128)}, u32[]{:S(2)}) copy-start(f32[16,256]{1,0:T(8,128)} %constant.34.clone.cos_y) | copy-start | bytes 49156
  2.5 22.2 %copy-start.7 = (bf16[512,256]{1,0:T(8,128)(2,1)S(1)}, bf16[512,256]{1,0:T(8,128)(2,1)}, u32[]{:S(2)}) copy-start(bf16[512,256]{1,0:T(8,128)(2,1)} %constant.37.clone.low) | copy-start | bytes 786436
  2.5 22.2 %copy-start.8 = (bf16[512,256]{1,0:T(8,128)(2,1)S(1)}, bf16[512,256]{1,0:T(8,128)(2,1)}, u32[]{:S(2)}) copy-start(bf16[512,256]{1,0:T(8,128)(2,1)} %constant.36.clone.high) | copy-start | bytes 786436
  24.8 39.5 %copy-start.4 = (f32[512,128]{1,0:T(8,128)S(1)}, f32[512,128]{1,0:T(8,128)}, u32[]{:S(2)}) copy-start(f32[512,128]{1,0:T(8,128)} %constant.44.clone.decay) | copy-start | bytes 786436
  24.8 39.5 %copy-start.9 = (f32[256,128]{1,0:T(8,128)S(1)}, f32[256,128]{1,0:T(8,128)}, u32[]{:S(2)}) copy-start(f32[256,128]{1,0:T(8,128)} %constant.39.clone.sin_c) | copy-start | bytes 393220
  24.8 39.4 %copy-start.10 = (f32[256,128]{1,0:T(8,128)S(1)}, f32[256,128]{1,0:T(8,128)}, u32[]{:S(2)}) copy-start(f32[256,128]{1,0:T(8,128)} %constant.38.clone.cos_c) | copy-start | bytes 393220
  24.8 39.4 %copy-start.15 = (f32[32,128]{1,0:T(8,128)S(1)}, f32[32,128]{1,0:T(8,128)}, u32[]{:S(2)}) copy-start(f32[32,128]{1,0:T(8,128)} %constant.41.clone.sin_r) | copy-start | bytes 49156
  24.8 39.4 %copy-start.16 = (f32[32,128]{1,0:T(8,128)S(1)}, f32[32,128]{1,0:T(8,128)}, u32[]{:S(2)}) copy-start(f32[32,128]{1,0:T(8,128)} %constant.40.clone.cos_r) | copy-start | bytes 49156
  24.8 39.4 %copy-start.17 = (f32[16,128]{1,0:T(8,128)S(1)}, f32[16,128]{1,0:T(8,128)}, u32[]{:S(2)}) copy-start(f32[16,128]{1,0:T(8,128)} %constant.43.clone.sin_k) | copy-start | bytes 24580
  24.8 39.4 %copy-start.18 = (f32[16,128]{1,0:T(8,128)S(1)}, f32[16,128]{1,0:T(8,128)}, u32[]{:S(2)}) copy-start(f32[16,128]{1,0:T(8,128)} %constant.42.clone.cos_k) | copy-start | bytes 24580
  25.9 38.4 %copy-start = (bf16[512,256]{1,0:T(8,128)(2,1)S(1)}, bf16[512,256]{1,0:T(8,128)(2,1)}, u32[]{:S(2)}) copy-start(bf16[512,256]{1,0:T(8,128)(2,1)} %constant.48.clone.bl) | copy-start | bytes 786436
  25.9 38.4 %copy-start.1 = (bf16[512,256]{1,0:T(8,128)(2,1)S(1)}, bf16[512,256]{1,0:T(8,128)(2,1)}, u32[]{:S(2)}) copy-start(bf16[512,256]{1,0:T(8,128)(2,1)} %constant.47.clone.bh) | copy-start | bytes 786436
  25.9 38.4 %copy-start.2 = (bf16[256,512]{1,0:T(8,128)(2,1)S(1)}, bf16[256,512]{1,0:T(8,128)(2,1)}, u32[]{:S(2)}) copy-start(bf16[256,512]{1,0:T(8,128)(2,1)} %constant.46.clone.fl) | copy-start | bytes 786436
  26.0 38.3 %copy-start.3 = (bf16[256,512]{1,0:T(8,128)(2,1)S(1)}, bf16[256,512]{1,0:T(8,128)(2,1)}, u32[]{:S(2)}) copy-start(bf16[256,512]{1,0:T(8,128)(2,1)} %constant.45.clone.fh) | copy-start | bytes 786436
  66.0 26.1 %copy-start.5 = (bf16[256,512]{1,0:T(8,128)(2,1)S(1)}, bf16[256,512]{1,0:T(8,128)(2,1)}, u32[]{:S(2)}) copy-start(bf16[256,512]{1,0:T(8,128)(2,1)} %constant.50.clone.low) | copy-start | bytes 786436
  66.0 26.1 %copy-start.6 = (bf16[256,512]{1,0:T(8,128)(2,1)S(1)}, bf16[256,512]{1,0:T(8,128)(2,1)}, u32[]{:S(2)}) copy-start(bf16[256,512]{1,0:T(8,128)(2,1)} %constant.49.clone.high) | copy-start | bytes 786436

commit v7 on v4

--- a/solution.py
+++ b/solution.py
@@ -151,8 +151,9 @@
 
 
 def x_section(
-    place, lines, cos_c, sin_c, cos_r, sin_r, cos_k, sin_k, decay, fh, fl, bh, bl, out, a_re, a_im, cos_i, sin_i, wide, gh, gl, late_c, late_s
+    lines, cos_c, sin_c, cos_r, sin_r, cos_k, sin_k, decay, fh, fl, bh, bl, out, a_re, a_im, cos_i, sin_i, wide, gh, gl, late_c, late_s
 ):
+    place = lax.axis_index(ROW), lax.axis_index("col")
     for part in range(2):
         for slot in range(4):
             here = slice(LANES * part + 32 * slot, LANES * part + 32 * (slot + 1))
@@ -330,12 +331,11 @@
     return -diffusion * (angular * angular) - decay, jnp.where(substrate, -normalize, normalize)
 
 
-def call(body, out_shape, scratch, *operands, scalars=0):
-    spaces = [pl.BlockSpec(memory_space=pltpu.SMEM if k < scalars else pltpu.VMEM) for k in range(len(operands))]
+def call(body, out_shape, scratch, *operands):
     return pl.pallas_call(
         body,
         out_shape=jax.ShapeDtypeStruct(out_shape, jnp.float32),
-        in_specs=spaces,
+        in_specs=[pl.BlockSpec(memory_space=pltpu.VMEM) for _ in operands],
         out_specs=pl.BlockSpec(memory_space=pltpu.VMEM),
         scratch_shapes=[pltpu.VMEM(shape[:2], *shape[2:] or (jnp.float32,)) for shape in scratch],
         compiler_params=pltpu.CompilerParams(vmem_limit_bytes=48 * 1024 * 1024),
@@ -344,15 +344,13 @@
 
 def on_device(substrate, activator):
     along_y, along_x, back_y = tables()
-    place = jnp.stack([lax.axis_index(ROW), lax.axis_index("col")])
     fields = jnp.concatenate([substrate.reshape(C, I, M), activator.reshape(C, I, M)], axis=1)
-    fields, place = lax.optimization_barrier((fields, place))
     fields = lax.all_to_all(fields, "col", 0, 0, tiled=True)
     pieces = call(y_forward, (2 * D, LANES), [(D, 2 * M)], fields, *along_y)
     lines = lax.all_to_all(pieces.reshape(D, 2, LANES), ALL, 0, 0, tiled=True).reshape(2 * D, LANES)
     scratch = [(24 * R, LANES)] * 2 + [(D, LANES)] * 2 + [(D, 2 * LANES)]
     scratch += [(2 * LANES, 4 * LANES, jnp.bfloat16)] * 2 + [(7 * R, LANES)] * 2
-    pieces = call(x_section, (D, LANES), scratch, place, lines, *along_x, scalars=1)
+    pieces = call(x_section, (D, LANES), scratch, lines, *along_x)
     pieces = lax.all_to_all(pieces.reshape(D, 1, LANES), ALL, 0, 0, tiled=True).reshape(D, LANES)
     fields = call(y_backward, (C, 2 * I, M), [(M, M), (M, 2 * M)], pieces, *back_y)
     fields = lax.all_to_all(fields, "col", 0, 0, tiled=True)

time: 109 us -> 108 us (level)
  no operation moved by 1% of the time
where the time goes in v7:
time: 108 us; the launch traced here: 107 us
  blocking collectives  101 us (94%)
  Pallas kernels  3.38 us (3%)
    all_to_all x1, blocking collectives, on_device(): lax.all_to_all(pieces.reshape(D, 2, LANES), ALL, 0, 0, tiled=True)  38.3 us
    all_to_all x2, blocking collectives, on_device(): fields = lax.all_to_all(fields, 'col', 0, 0, tiled=True)  37.1 us
    all_to_all x1, blocking collectives, on_device(): lax.all_to_all(pieces.reshape(D, 1, LANES), ALL, 0, 0, tiled=True)  26.1 us
    pallas_call x3, Pallas kernels, call(): pl.pallas_call(body, out_shape=jax.ShapeDtypeStruct(out_shape, jnp.float3...  3.38 us

profile of v7, /device:TPU:1, one launch (start us, length us, event | category | flops | bytes accessed | tf_op | source)
XLA Modules:
  0.0 107.5 jit_solution(2277266259534546280)
XLA Ops:
  0.6 0.0 copy-start.11
  0.6 0.0 copy-start.12
  0.7 1.0 pad_maximum_fusion
  1.7 0.0 copy-start.7
  1.7 0.0 copy-start.8
  1.7 22.2 %all_to_all.20.fields = f32[16,16,256]{2,1,0:T(8,128)S(1)} all-to-all(f32[16,16,256]{2,1,0:T(8,128)S(1)} %pad_maximum_fusion), channel_id=1, replica_groups=mesh['row_0'=8,'row_1'=2,'row_2'=2,'col'=16] {'col'}, dimensions={0} | all-to-all | bytes 524288 | tf_op jit(solution)/shard_map/all_to_all | solution.py:348
  23.9 0.0 copy-start.4
  23.9 0.0 copy-start.9
  23.9 0.0 copy-start.10
  23.9 0.0 copy-start.13
  24.0 0.0 copy-start.15
  24.0 0.0 copy-start.16
  24.0 1.1 shard_map.194
  25.1 0.0 copy-start
  25.1 0.0 copy-start.1
  25.1 0.0 copy-start.2
  25.1 0.0 copy-start.3
  25.1 38.3 %all_to_all.21 = f32[512,2,128]{2,1,0:T(2,128)S(1)} all-to-all(f32[512,2,128]{2,1,0:T(2,128)S(1)} %bitcast.13), channel_id=1, replica_groups=mesh['row_0'=8,'row_1'=2,'row_2'=2,'col'=16] {'row_0','row_1','row_2','c..., dimensions={0} | all-to-all | bytes 1048576 | tf_op jit(solution)/shard_map/all_to_all | solution.py:350
  63.5 1.7 %shard_map.195 = f32[512,128]{1,0:T(8,128)S(1)} custom-call(f32[1024,128]{1,0:T(8,128)S(1)} %bitcast.12, f32[256,128]{1,0:T(8,128)S(1)} %copy-done.10, f32[256,128]{1,0:T(8,128)S(1)} %copy-done.9, f32[32,128]{1,0:T(8,128)S(1)} %copy-done.14, f32[32,128]{1,0:T(8,128)S(1)} %copy-done.13, f32[16,128]{1,0:T(8,128)S(1)} %copy-done.16, f32[16,128]{1,0:T(8,128)S(1)} %copy-done.15, ...), custom_call_target="tpu_custom_call" | custom-call | tf_op jit(solution)/shard_map/pallas_call | solution.py:335
  65.2 0.0 copy-start.6
  65.2 26.1 %all_to_all.22 = f32[512,1,128]{2,1,0:T(1,128)S(1)} all-to-all(f32[512,1,128]{2,1,0:T(1,128)S(1)} %bitcast.14), channel_id=1, replica_groups=mesh['row_0'=8,'row_1'=2,'row_2'=2,'col'=16] {'row_0','row_1','row_2','c..., dimensions={0} | all-to-all | bytes 524288 | tf_op jit(solution)/shard_map/all_to_all | solution.py:354
  91.2 0.6 shard_map.196
  91.9 14.9 %all_to_all.23 = f32[16,16,256]{2,1,0:T(8,128)S(1)} all-to-all(f32[16,16,256]{2,1,0:T(8,128)S(1)} %shard_map.196), channel_id=1, replica_groups=mesh['row_0'=8,'row_1'=2,'row_2'=2,'col'=16] {'col'}, dimensions={0} | all-to-all | bytes 524288 | tf_op jit(solution)/shard_map/all_to_all | solution.py:356
  106.8 0.7 slice_bitcast_fusion
  (19 shorter events, 0.0 us)
Async XLA Ops:
  0.6 23.3 %copy-start.11 = (f32[16,256]{1,0:T(8,128)S(1)}, f32[16,256]{1,0:T(8,128)}, u32[]{:S(2)}) copy-start(f32[16,256]{1,0:T(8,128)} %constant.35.clone.sin_y) | copy-start | bytes 49156
  0.6 23.3 %copy-start.12 = (f32[16,256]{1,0:T(8,128)S(1)}, f32[16,256]{1,0:T(8,128)}, u32[]{:S(2)}) copy-start(f32[16,256]{1,0:T(8,128)} %constant.34.clone.cos_y) | copy-start | bytes 49156
  1.7 22.2 %copy-start.7 = (bf16[512,256]{1,0:T(8,128)(2,1)S(1)}, bf16[512,256]{1,0:T(8,128)(2,1)}, u32[]{:S(2)}) copy-start(bf16[512,256]{1,0:T(8,128)(2,1)} %constant.37.clone.low) | copy-start | bytes 786436
  1.7 22.2 %copy-start.8 = (bf16[512,256]{1,0:T(8,128)(2,1)S(1)}, bf16[512,256]{1,0:T(8,128)(2,1)}, u32[]{:S(2)}) copy-start(bf16[512,256]{1,0:T(8,128)(2,1)} %constant.36.clone.high) | copy-start | bytes 786436
  23.9 39.5 %copy-start.4 = (f32[512,128]{1,0:T(8,128)S(1)}, f32[512,128]{1,0:T(8,128)}, u32[]{:S(2)}) copy-start(f32[512,128]{1,0:T(8,128)} %constant.44.clone.decay) | copy-start | bytes 786436
  23.9 39.5 %copy-start.9 = (f32[256,128]{1,0:T(8,128)S(1)}, f32[256,128]{1,0:T(8,128)}, u32[]{:S(2)}) copy-start(f32[256,128]{1,0:T(8,128)} %constant.39.clone.sin_c) | copy-start | bytes 393220
  23.9 39.4 %copy-start.10 = (f32[256,128]{1,0:T(8,128)S(1)}, f32[256,128]{1,0:T(8,128)}, u32[]{:S(2)}) copy-start(f32[256,128]{1,0:T(8,128)} %constant.38.clone.cos_c) | copy-start | bytes 393220
  23.9 39.4 %copy-start.13 = (f32[32,128]{1,0:T(8,128)S(1)}, f32[32,128]{1,0:T(8,128)}, u32[]{:S(2)}) copy-start(f32[32,128]{1,0:T(8,128)} %constant.41.clone.sin_r) | copy-start | bytes 49156
  24.0 39.4 %copy-start.14 = (f32[32,128]{1,0:T(8,128)S(1)}, f32[32,128]{1,0:T(8,128)}, u32[]{:S(2)}) copy-start(f32[32,128]{1,0:T(8,128)} %constant.40.clone.cos_r) | copy-start | bytes 49156
  24.0 39.4 %copy-start.15 = (f32[16,128]{1,0:T(8,128)S(1)}, f32[16,128]{1,0:T(8,128)}, u32[]{:S(2)}) copy-start(f32[16,128]{1,0:T(8,128)} %constant.43.clone.sin_k) | copy-start | bytes 24580
  24.0 39.4 %copy-start.16 = (f32[16,128]{1,0:T(8,128)S(1)}, f32[16,128]{1,0:T(8,128)}, u32[]{:S(2)}) copy-start(f32[16,128]{1,0:T(8,128)} %constant.42.clone.cos_k) | copy-start | bytes 24580
  25.1 38.4 %copy-start = (bf16[512,256]{1,0:T(8,128)(2,1)S(1)}, bf16[512,256]{1,0:T(8,128)(2,1)}, u32[]{:S(2)}) copy-start(bf16[512,256]{1,0:T(8,128)(2,1)} %constant.48.clone.bl) | copy-start | bytes 786436
  25.1 38.4 %copy-start.1 = (bf16[512,256]{1,0:T(8,128)(2,1)S(1)}, bf16[512,256]{1,0:T(8,128)(2,1)}, u32[]{:S(2)}) copy-start(bf16[512,256]{1,0:T(8,128)(2,1)} %constant.47.clone.bh) | copy-start | bytes 786436
  25.1 38.4 %copy-start.2 = (bf16[256,512]{1,0:T(8,128)(2,1)S(1)}, bf16[256,512]{1,0:T(8,128)(2,1)}, u32[]{:S(2)}) copy-start(bf16[256,512]{1,0:T(8,128)(2,1)} %constant.46.clone.fl) | copy-start | bytes 786436
  25.1 38.3 %copy-start.3 = (bf16[256,512]{1,0:T(8,128)(2,1)S(1)}, bf16[256,512]{1,0:T(8,128)(2,1)}, u32[]{:S(2)}) copy-start(bf16[256,512]{1,0:T(8,128)(2,1)} %constant.45.clone.fh) | copy-start | bytes 786436
  65.2 26.1 %copy-start.5 = (bf16[256,512]{1,0:T(8,128)(2,1)S(1)}, bf16[256,512]{1,0:T(8,128)(2,1)}, u32[]{:S(2)}) copy-start(bf16[256,512]{1,0:T(8,128)(2,1)} %constant.50.clone.low) | copy-start | bytes 786436
  65.2 26.1 %copy-start.6 = (bf16[256,512]{1,0:T(8,128)(2,1)S(1)}, bf16[256,512]{1,0:T(8,128)(2,1)}, u32[]{:S(2)}) copy-start(bf16[256,512]{1,0:T(8,128)(2,1)} %constant.49.clone.high) | copy-start | bytes 786436

commit v8 on v5

--- a/solution.py
+++ b/solution.py
@@ -156,8 +156,9 @@
 
 
 def x_section(
-    place, lines, cos_c, sin_c, cos_r, sin_r, cos_k, sin_k, decay, fh, fl, bh, bl, out, a_re, a_im, cos_i, sin_i, wide, gh, gl, late_c, late_s
+    lines, cos_c, sin_c, cos_r, sin_r, cos_k, sin_k, decay, fh, fl, bh, bl, out, a_re, a_im, cos_i, sin_i, wide, gh, gl, late_c, late_s
 ):
+    place = lax.axis_index(ROW_BY_CORE), lax.axis_index("col")
     for part in range(2):
         for slot in range(4):
             here = slice(LANES * part + 32 * slot, LANES * part + 32 * (slot + 1))
@@ -337,12 +338,11 @@
     return -diffusion * (angular * angular) - decay, jnp.where(substrate, -normalize, normalize)
 
 
-def call(body, out_shape, scratch, *operands, scalars=0):
-    spaces = [pl.BlockSpec(memory_space=pltpu.SMEM if k < scalars else pltpu.VMEM) for k in range(len(operands))]
+def call(body, out_shape, scratch, *operands):
     return pl.pallas_call(
         body,
         out_shape=jax.ShapeDtypeStruct(out_shape, jnp.float32),
-        in_specs=spaces,
+        in_specs=[pl.BlockSpec(memory_space=pltpu.VMEM) for _ in operands],
         out_specs=pl.BlockSpec(memory_space=pltpu.VMEM),
         scratch_shapes=[pltpu.VMEM(shape[:2], *shape[2:] or (jnp.float32,)) for shape in scratch],
         compiler_params=pltpu.CompilerParams(vmem_limit_bytes=48 * 1024 * 1024),
@@ -351,15 +351,13 @@
 
 def on_device(substrate, activator):
     along_y, along_x, back_y = tables()
-    place = jnp.stack([lax.axis_index(ROW_BY_CORE), lax.axis_index("col")])
     fields = jnp.concatenate([substrate.reshape(C, I, M), activator.reshape(C, I, M)], axis=1)
-    fields, place = lax.optimization_barrier((fields, place))
     fields = lax.all_to_all(fields, "col", 0, 0, tiled=True)
     pieces = call(y_forward, (2 * D, LANES), [(D, 2 * M)], fields, *along_y)
     lines = lax.all_to_all(pieces.reshape(D, 2, LANES), ALL, 0, 0, tiled=True).reshape(2 * D, LANES)
     scratch = [(24 * R, LANES)] * 2 + [(D, LANES)] * 2 + [(D, 2 * LANES)]
     scratch += [(2 * LANES, 4 * LANES, jnp.bfloat16)] * 2 + [(7 * R, LANES)] * 2
-    pieces = call(x_section, (D, LANES), scratch, place, lines, *along_x, scalars=1)
+    pieces = call(x_section, (D, LANES), scratch, lines, *along_x)
     pieces = lax.all_to_all(pieces.reshape(D, 1, LANES), ALL, 0, 0, tiled=True).reshape(D, LANES)
     fields = call(y_backward, (C, 2 * I, M), [(M, M), (M, 2 * M)], pieces, *back_y)
     fields = lax.all_to_all(fields, "col", 0, 0, tiled=True)

time: 109 us -> 108 us (level)
  no operation moved by 1% of the time
where the time goes in v8:
time: 108 us
  blocking collectives  102 us (94%)
  Pallas kernels  3.38 us (3%)
    all_to_all x1, blocking collectives, on_device(): lax.all_to_all(pieces.reshape(D, 2, LANES), ALL, 0, 0, tiled=True)  38.5 us
    all_to_all x2, blocking collectives, on_device(): fields = lax.all_to_all(fields, 'col', 0, 0, tiled=True)  37.4 us
    all_to_all x1, blocking collectives, on_device(): lax.all_to_all(pieces.reshape(D, 1, LANES), ALL, 0, 0, tiled=True)  25.9 us
    pallas_call x3, Pallas kernels, call(): pl.pallas_call(body, out_shape=jax.ShapeDtypeStruct(out_shape, jnp.float3...  3.38 us

profile of v8, /device:TPU:1, one launch (start us, length us, event | category | flops | bytes accessed | tf_op | source)
XLA Modules:
  0.0 107.8 jit_solution(12415622987937543135)
XLA Ops:
  0.6 0.0 copy-start.11
  0.6 0.0 copy-start.12
  0.7 1.0 pad_maximum_fusion
  1.7 0.0 copy-start.7
  1.7 0.0 copy-start.8
  1.7 22.2 %all_to_all.20.fields = f32[16,16,256]{2,1,0:T(8,128)S(1)} all-to-all(f32[16,16,256]{2,1,0:T(8,128)S(1)} %pad_maximum_fusion), channel_id=1, replica_groups=mesh['row_0'=8,'row_1'=2,'row_2'=2,'col'=16] {'col'}, dimensions={0} | all-to-all | bytes 524288 | tf_op jit(solution)/shard_map/all_to_all | solution.py:355
  23.9 0.0 copy-start.4
  23.9 0.0 copy-start.9
  23.9 0.0 copy-start.13
  24.0 0.0 copy-start.14
  24.0 0.0 copy-start.15
  24.0 0.0 copy-start.16
  24.0 1.1 shard_map.194
  25.1 0.0 copy-start
  25.1 0.0 copy-start.1
  25.1 0.0 copy-start.2
  25.1 0.0 copy-start.3
  25.1 38.5 %all_to_all.21 = f32[512,2,128]{2,1,0:T(2,128)S(1)} all-to-all(f32[512,2,128]{2,1,0:T(2,128)S(1)} %bitcast.13), channel_id=1, replica_groups=mesh['row_0'=8,'row_1'=2,'row_2'=2,'col'=16] {'row_2','row_0','row_1','c..., dimensions={0} | all-to-all | bytes 1048576 | tf_op jit(solution)/shard_map/all_to_all | solution.py:357
  63.7 1.7 %shard_map.195 = f32[512,128]{1,0:T(8,128)S(1)} custom-call(f32[1024,128]{1,0:T(8,128)S(1)} %bitcast.12, f32[256,128]{1,0:T(8,128)S(1)} %copy-done.10, f32[256,128]{1,0:T(8,128)S(1)} %copy-done.9, f32[32,128]{1,0:T(8,128)S(1)} %copy-done.14, f32[32,128]{1,0:T(8,128)S(1)} %copy-done.13, f32[16,128]{1,0:T(8,128)S(1)} %copy-done.16, f32[16,128]{1,0:T(8,128)S(1)} %copy-done.15, ...), custom_call_target="tpu_custom_call" | custom-call | tf_op jit(solution)/shard_map/pallas_call | solution.py:342
  65.4 0.0 copy-start.6
  65.4 25.9 %all_to_all.22 = f32[512,1,128]{2,1,0:T(1,128)S(1)} all-to-all(f32[512,1,128]{2,1,0:T(1,128)S(1)} %bitcast.14), channel_id=1, replica_groups=mesh['row_0'=8,'row_1'=2,'row_2'=2,'col'=16] {'row_2','row_0','row_1','c..., dimensions={0} | all-to-all | bytes 524288 | tf_op jit(solution)/shard_map/all_to_all | solution.py:361
  91.3 0.6 shard_map.196
  91.9 15.2 %all_to_all.23 = f32[16,16,256]{2,1,0:T(8,128)S(1)} all-to-all(f32[16,16,256]{2,1,0:T(8,128)S(1)} %shard_map.196), channel_id=1, replica_groups=mesh['row_0'=8,'row_1'=2,'row_2'=2,'col'=16] {'col'}, dimensions={0} | all-to-all | bytes 524288 | tf_op jit(solution)/shard_map/all_to_all | solution.py:363
  107.1 0.7 slice_bitcast_fusion
  (19 shorter events, 0.0 us)
Async XLA Ops:
  0.6 23.3 %copy-start.11 = (f32[16,256]{1,0:T(8,128)S(1)}, f32[16,256]{1,0:T(8,128)}, u32[]{:S(2)}) copy-start(f32[16,256]{1,0:T(8,128)} %constant.35.clone.sin_y) | copy-start | bytes 49156
  0.6 23.3 %copy-start.12 = (f32[16,256]{1,0:T(8,128)S(1)}, f32[16,256]{1,0:T(8,128)}, u32[]{:S(2)}) copy-start(f32[16,256]{1,0:T(8,128)} %constant.34.clone.cos_y) | copy-start | bytes 49156
  1.7 22.2 %copy-start.7 = (bf16[512,256]{1,0:T(8,128)(2,1)S(1)}, bf16[512,256]{1,0:T(8,128)(2,1)}, u32[]{:S(2)}) copy-start(bf16[512,256]{1,0:T(8,128)(2,1)} %constant.37.clone.low) | copy-start | bytes 786436
  1.7 22.2 %copy-start.8 = (bf16[512,256]{1,0:T(8,128)(2,1)S(1)}, bf16[512,256]{1,0:T(8,128)(2,1)}, u32[]{:S(2)}) copy-start(bf16[512,256]{1,0:T(8,128)(2,1)} %constant.36.clone.high) | copy-start | bytes 786436
  23.9 39.7 %copy-start.4 = (f32[512,128]{1,0:T(8,128)S(1)}, f32[512,128]{1,0:T(8,128)}, u32[]{:S(2)}) copy-start(f32[512,128]{1,0:T(8,128)} %constant.44.clone.decay) | copy-start | bytes 786436
  23.9 39.7 %copy-start.9 = (f32[256,128]{1,0:T(8,128)S(1)}, f32[256,128]{1,0:T(8,128)}, u32[]{:S(2)}) copy-start(f32[256,128]{1,0:T(8,128)} %constant.39.clone.sin_c) | copy-start | bytes 393220
  23.9 39.7 %copy-start.10 = (f32[256,128]{1,0:T(8,128)S(1)}, f32[256,128]{1,0:T(8,128)}, u32[]{:S(2)}) copy-start(f32[256,128]{1,0:T(8,128)} %constant.38.clone.cos_c) | copy-start | bytes 393220
  23.9 39.7 %copy-start.13 = (f32[32,128]{1,0:T(8,128)S(1)}, f32[32,128]{1,0:T(8,128)}, u32[]{:S(2)}) copy-start(f32[32,128]{1,0:T(8,128)} %constant.41.clone.sin_r) | copy-start | bytes 49156
  24.0 39.7 %copy-start.14 = (f32[32,128]{1,0:T(8,128)S(1)}, f32[32,128]{1,0:T(8,128)}, u32[]{:S(2)}) copy-start(f32[32,128]{1,0:T(8,128)} %constant.40.clone.cos_r) | copy-start | bytes 49156
  24.0 39.7 %copy-start.15 = (f32[16,128]{1,0:T(8,128)S(1)}, f32[16,128]{1,0:T(8,128)}, u32[]{:S(2)}) copy-start(f32[16,128]{1,0:T(8,128)} %constant.43.clone.sin_k) | copy-start | bytes 24580
  24.0 39.7 %copy-start.16 = (f32[16,128]{1,0:T(8,128)S(1)}, f32[16,128]{1,0:T(8,128)}, u32[]{:S(2)}) copy-start(f32[16,128]{1,0:T(8,128)} %constant.42.clone.cos_k) | copy-start | bytes 24580
  25.1 38.6 %copy-start = (bf16[512,256]{1,0:T(8,128)(2,1)S(1)}, bf16[512,256]{1,0:T(8,128)(2,1)}, u32[]{:S(2)}) copy-start(bf16[512,256]{1,0:T(8,128)(2,1)} %constant.48.clone.bl) | copy-start | bytes 786436
  25.1 38.6 %copy-start.1 = (bf16[512,256]{1,0:T(8,128)(2,1)S(1)}, bf16[512,256]{1,0:T(8,128)(2,1)}, u32[]{:S(2)}) copy-start(bf16[512,256]{1,0:T(8,128)(2,1)} %constant.47.clone.bh) | copy-start | bytes 786436
  25.1 38.6 %copy-start.2 = (bf16[256,512]{1,0:T(8,128)(2,1)S(1)}, bf16[256,512]{1,0:T(8,128)(2,1)}, u32[]{:S(2)}) copy-start(bf16[256,512]{1,0:T(8,128)(2,1)} %constant.46.clone.fl) | copy-start | bytes 786436
  25.1 38.6 %copy-start.3 = (bf16[256,512]{1,0:T(8,128)(2,1)S(1)}, bf16[256,512]{1,0:T(8,128)(2,1)}, u32[]{:S(2)}) copy-start(bf16[256,512]{1,0:T(8,128)(2,1)} %constant.45.clone.fh) | copy-start | bytes 786436
  65.4 25.9 %copy-start.5 = (bf16[256,512]{1,0:T(8,128)(2,1)S(1)}, bf16[256,512]{1,0:T(8,128)(2,1)}, u32[]{:S(2)}) copy-start(bf16[256,512]{1,0:T(8,128)(2,1)} %constant.50.clone.low) | copy-start | bytes 786436
  65.4 25.9 %copy-start.6 = (bf16[256,512]{1,0:T(8,128)(2,1)S(1)}, bf16[256,512]{1,0:T(8,128)(2,1)}, u32[]{:S(2)}) copy-start(bf16[256,512]{1,0:T(8,128)(2,1)} %constant.49.clone.high) | copy-start | bytes 786436

commit v9 on v7

--- a/solution.py
+++ b/solution.py
@@ -196,7 +196,7 @@
             cos_i[rows, :], sin_i[rows, :] = u, v
             wide[rows, :LANES] = re * u + im * v
             wide[rows, LANES:] = im * u - re * v
-    along_y, normal = column_factors(place)
+    along_y = column_factors(place)
     low_lanes = lane_of((8, LANES)) < 64
     for g in range(2):
         advanced = []
@@ -205,7 +205,7 @@
             spectra = dot(halves(wide[rows, :]), (gh[...], gl[...]))
             linear = decay[rows, :] + along_y
             grown = jnp.exp(linear * (0.5 * TIME_STEP))
-            growth, forcing = grown * (1.0 / (N * N)), (grown - 1.0) / linear * normal
+            growth, forcing = grown, (grown - 1.0) / linear
             advanced.append(growth * spectra[:, :LANES] + forcing * spectra[:, 2 * LANES : 3 * LANES])
             advanced.append(growth * spectra[:, LANES : 2 * LANES] + forcing * spectra[:, 3 * LANES :])
         both = dot(halves(jnp.concatenate(advanced, axis=1)), (bh[...], bl[...]))
@@ -297,8 +297,10 @@
                 there = slice(start, start + I)
                 forward[0, there, kind, 0, here], forward[1, there, kind, 0, here] = c, s
                 forward[0, there, kind, 1, here], forward[1, there, kind, 1, here] = -s, c
+    for slot in range(5):
+        forward[:, :, 1, :, 16 * slot : 16 * slot + I] *= -1
     forward = forward.reshape(2 * LANES, 4 * LANES)
-    backward = backward.reshape(4 * LANES, 2 * LANES)
+    backward = backward.reshape(4 * LANES, 2 * LANES) / (N * N)
     lane = np.arange(LANES)[None, :]
     row = np.arange(D)[:, None]
     p = 8 * (row // LANES) + row % 8 + R * (row % LANES // 8) + D * (lane % I)
@@ -327,8 +329,7 @@
     substrate = (lane & I) == 0
     diffusion = jnp.where(substrate, SUBSTRATE_DIFFUSION, ACTIVATOR_DIFFUSION)
     decay = jnp.where(substrate, FEED_RATE, FEED_RATE + KILL_RATE)
-    normalize = 1.0 / (N * N)
-    return -diffusion * (angular * angular) - decay, jnp.where(substrate, -normalize, normalize)
+    return -diffusion * (angular * angular) - decay
 
 
 def call(body, out_shape, scratch, *operands):

time: 108 us -> 108 us (level)
  no operation moved by 1% of the time
where the time goes in v9:
time: 108 us; the launch traced here: 107 us
  blocking collectives  101 us (94%)
  Pallas kernels  3.38 us (3%)
    all_to_all x1, blocking collectives, on_device(): lax.all_to_all(pieces.reshape(D, 2, LANES), ALL, 0, 0, tiled=True)  38.3 us
    all_to_all x2, blocking collectives, on_device(): fields = lax.all_to_all(fields, 'col', 0, 0, tiled=True)  37.1 us
    all_to_all x1, blocking collectives, on_device(): lax.all_to_all(pieces.reshape(D, 1, LANES), ALL, 0, 0, tiled=True)  26.1 us
    pallas_call x3, Pallas kernels, call(): pl.pallas_call(body, out_shape=jax.ShapeDtypeStruct(out_shape, jnp.float3...  3.38 us

profile of v9, /device:TPU:1, one launch (start us, length us, event | category | flops | bytes accessed | tf_op | source)
XLA Modules:
  0.0 107.5 jit_solution(11876365041530410857)
XLA Ops:
  0.6 0.0 copy-start.11
  0.6 0.0 copy-start.12
  0.7 1.0 pad_maximum_fusion
  1.7 0.0 copy-start.7
  1.7 0.0 copy-start.8
  1.7 22.2 %all_to_all.20.fields = f32[16,16,256]{2,1,0:T(8,128)S(1)} all-to-all(f32[16,16,256]{2,1,0:T(8,128)S(1)} %pad_maximum_fusion), channel_id=1, replica_groups=mesh['row_0'=8,'row_1'=2,'row_2'=2,'col'=16] {'col'}, dimensions={0} | all-to-all | bytes 524288 | tf_op jit(solution)/shard_map/all_to_all | solution.py:349
  23.9 0.0 copy-start.4
  23.9 0.0 copy-start.9
  23.9 0.0 copy-start.10
  23.9 0.0 copy-start.13
  24.0 0.0 copy-start.14
  24.0 0.0 copy-start.15
  24.0 1.1 shard_map.194
  25.1 0.0 copy-start
  25.1 0.0 copy-start.1
  25.1 0.0 copy-start.2
  25.1 0.0 copy-start.3
  25.1 38.3 %all_to_all.21 = f32[512,2,128]{2,1,0:T(2,128)S(1)} all-to-all(f32[512,2,128]{2,1,0:T(2,128)S(1)} %bitcast.13), channel_id=1, replica_groups=mesh['row_0'=8,'row_1'=2,'row_2'=2,'col'=16] {'row_0','row_1','row_2','c..., dimensions={0} | all-to-all | bytes 1048576 | tf_op jit(solution)/shard_map/all_to_all | solution.py:351
  63.5 1.7 %shard_map.195 = f32[512,128]{1,0:T(8,128)S(1)} custom-call(f32[1024,128]{1,0:T(8,128)S(1)} %bitcast.12, f32[256,128]{1,0:T(8,128)S(1)} %copy-done.10, f32[256,128]{1,0:T(8,128)S(1)} %copy-done.9, f32[32,128]{1,0:T(8,128)S(1)} %copy-done.14, f32[32,128]{1,0:T(8,128)S(1)} %copy-done.13, f32[16,128]{1,0:T(8,128)S(1)} %copy-done.16, f32[16,128]{1,0:T(8,128)S(1)} %copy-done.15, ...), custom_call_target="tpu_custom_call" | custom-call | tf_op jit(solution)/shard_map/pallas_call | solution.py:336
  65.2 0.0 copy-start.6
  65.2 26.1 %all_to_all.22 = f32[512,1,128]{2,1,0:T(1,128)S(1)} all-to-all(f32[512,1,128]{2,1,0:T(1,128)S(1)} %bitcast.14), channel_id=1, replica_groups=mesh['row_0'=8,'row_1'=2,'row_2'=2,'col'=16] {'row_0','row_1','row_2','c..., dimensions={0} | all-to-all | bytes 524288 | tf_op jit(solution)/shard_map/all_to_all | solution.py:355
  91.2 0.6 shard_map.196
  91.9 14.9 %all_to_all.23 = f32[16,16,256]{2,1,0:T(8,128)S(1)} all-to-all(f32[16,16,256]{2,1,0:T(8,128)S(1)} %shard_map.196), channel_id=1, replica_groups=mesh['row_0'=8,'row_1'=2,'row_2'=2,'col'=16] {'col'}, dimensions={0} | all-to-all | bytes 524288 | tf_op jit(solution)/shard_map/all_to_all | solution.py:357
  106.8 0.7 slice_bitcast_fusion
  (19 shorter events, 0.0 us)
Async XLA Ops:
  0.6 23.3 %copy-start.11 = (f32[16,256]{1,0:T(8,128)S(1)}, f32[16,256]{1,0:T(8,128)}, u32[]{:S(2)}) copy-start(f32[16,256]{1,0:T(8,128)} %constant.35.clone.sin_y) | copy-start | bytes 49156
  0.6 23.3 %copy-start.12 = (f32[16,256]{1,0:T(8,128)S(1)}, f32[16,256]{1,0:T(8,128)}, u32[]{:S(2)}) copy-start(f32[16,256]{1,0:T(8,128)} %constant.34.clone.cos_y) | copy-start | bytes 49156
  1.7 22.2 %copy-start.7 = (bf16[512,256]{1,0:T(8,128)(2,1)S(1)}, bf16[512,256]{1,0:T(8,128)(2,1)}, u32[]{:S(2)}) copy-start(bf16[512,256]{1,0:T(8,128)(2,1)} %constant.37.clone.low) | copy-start | bytes 786436
  1.7 22.2 %copy-start.8 = (bf16[512,256]{1,0:T(8,128)(2,1)S(1)}, bf16[512,256]{1,0:T(8,128)(2,1)}, u32[]{:S(2)}) copy-start(bf16[512,256]{1,0:T(8,128)(2,1)} %constant.36.clone.high) | copy-start | bytes 786436
  23.9 39.5 %copy-start.4 = (f32[512,128]{1,0:T(8,128)S(1)}, f32[512,128]{1,0:T(8,128)}, u32[]{:S(2)}) copy-start(f32[512,128]{1,0:T(8,128)} %constant.44.clone.decay) | copy-start | bytes 786436
  23.9 39.5 %copy-start.9 = (f32[256,128]{1,0:T(8,128)S(1)}, f32[256,128]{1,0:T(8,128)}, u32[]{:S(2)}) copy-start(f32[256,128]{1,0:T(8,128)} %constant.39.clone.sin_c) | copy-start | bytes 393220
  23.9 39.4 %copy-start.10 = (f32[256,128]{1,0:T(8,128)S(1)}, f32[256,128]{1,0:T(8,128)}, u32[]{:S(2)}) copy-start(f32[256,128]{1,0:T(8,128)} %constant.38.clone.cos_c) | copy-start | bytes 393220
  23.9 39.4 %copy-start.13 = (f32[32,128]{1,0:T(8,128)S(1)}, f32[32,128]{1,0:T(8,128)}, u32[]{:S(2)}) copy-start(f32[32,128]{1,0:T(8,128)} %constant.41.clone.sin_r) | copy-start | bytes 49156
  24.0 39.4 %copy-start.14 = (f32[32,128]{1,0:T(8,128)S(1)}, f32[32,128]{1,0:T(8,128)}, u32[]{:S(2)}) copy-start(f32[32,128]{1,0:T(8,128)} %constant.40.clone.cos_r) | copy-start | bytes 49156
  24.0 39.4 %copy-start.15 = (f32[16,128]{1,0:T(8,128)S(1)}, f32[16,128]{1,0:T(8,128)}, u32[]{:S(2)}) copy-start(f32[16,128]{1,0:T(8,128)} %constant.43.clone.sin_k) | copy-start | bytes 24580
  24.0 39.4 %copy-start.16 = (f32[16,128]{1,0:T(8,128)S(1)}, f32[16,128]{1,0:T(8,128)}, u32[]{:S(2)}) copy-start(f32[16,128]{1,0:T(8,128)} %constant.42.clone.cos_k) | copy-start | bytes 24580
  25.1 38.4 %copy-start = (bf16[512,256]{1,0:T(8,128)(2,1)S(1)}, bf16[512,256]{1,0:T(8,128)(2,1)}, u32[]{:S(2)}) copy-start(bf16[512,256]{1,0:T(8,128)(2,1)} %constant.48.clone.bl) | copy-start | bytes 786436
  25.1 38.4 %copy-start.1 = (bf16[512,256]{1,0:T(8,128)(2,1)S(1)}, bf16[512,256]{1,0:T(8,128)(2,1)}, u32[]{:S(2)}) copy-start(bf16[512,256]{1,0:T(8,128)(2,1)} %constant.47.clone.bh) | copy-start | bytes 786436
  25.1 38.4 %copy-start.2 = (bf16[256,512]{1,0:T(8,128)(2,1)S(1)}, bf16[256,512]{1,0:T(8,128)(2,1)}, u32[]{:S(2)}) copy-start(bf16[256,512]{1,0:T(8,128)(2,1)} %constant.46.clone.fl) | copy-start | bytes 786436
  25.1 38.3 %copy-start.3 = (bf16[256,512]{1,0:T(8,128)(2,1)S(1)}, bf16[256,512]{1,0:T(8,128)(2,1)}, u32[]{:S(2)}) copy-start(bf16[256,512]{1,0:T(8,128)(2,1)} %constant.45.clone.fh) | copy-start | bytes 786436
  65.2 26.1 %copy-start.5 = (bf16[256,512]{1,0:T(8,128)(2,1)S(1)}, bf16[256,512]{1,0:T(8,128)(2,1)}, u32[]{:S(2)}) copy-start(bf16[256,512]{1,0:T(8,128)(2,1)} %constant.50.clone.low) | copy-start | bytes 786436
  65.2 26.1 %copy-start.6 = (bf16[256,512]{1,0:T(8,128)(2,1)S(1)}, bf16[256,512]{1,0:T(8,128)(2,1)}, u32[]{:S(2)}) copy-start(bf16[256,512]{1,0:T(8,128)(2,1)} %constant.49.clone.high) | copy-start | bytes 786436
